TPU v7x, 128 devices: a whole 4x4x4 slice. The times are simulated.
128 devices in a mesh: fsdp: 8 (over x, z_lo), tenant: 8 (over y, z_hi), dp: 2 (over core).
Axes of the slice: x: 4, y: 4, z: 4 (z_hi: 2, z_lo: 2; z = z_hi * 2 + z_lo), core: 2. Of those that a mesh axis runs over, the one named last changes fastest.
Arguments:
- tokens: bfloat16 [6144, 5120], P(('fsdp', 'dp'), 'tenant'), may hold values from -6 to 6
- block_tenant_index: int32 [96], P(('fsdp', 'dp')), may hold values from 0 to 7
- ranks: int32 [8], replicated, may hold values from 16 to 64, as said below
- frozen_up_weight: bfloat16 [5120, 14336], P(('fsdp', 'dp'), 'tenant'), may hold values from -0.078125 to 0.078125
- tenant_down_adapters: bfloat16 [8, 64, 5120], P('tenant'), may hold values from -0.078125 to 0.078125
- tenant_up_adapters: bfloat16 [8, 64, 14336], P('tenant'), may hold values from -0.75 to 0.75
- cotangent: bfloat16 [6144, 14336], P(('fsdp', 'dp'), 'tenant'), may hold values from -6 to 6
Outputs:
- hidden_out: bfloat16 [6144, 14336], P(('fsdp', 'dp'), 'tenant')
- grad_tokens: bfloat16 [6144, 5120], P(('fsdp', 'dp'), 'tenant')
- grad_down: float32 [8, 64, 5120], P('dp', None, 'tenant')
- grad_up: float32 [8, 64, 14336], P('dp', None, 'tenant')
Inputs may be any that keep to these rules, and one draw needn't show every extreme that they name: `ranks`: multiples of 16; some tenant has rank 64.
All inputs are finite; a program needn't handle non-finite values.
Results may differ from a plain program's by a relative error of at most 0.0034.
Values may be sent and summed in bfloat16 or wider, within the bound.
A program may use at most 128 MiB of HBM per device.

v0:
```python
import jax
import jax.numpy as jnp
from jax import lax
from jax.sharding import PartitionSpec as P

BLOCK = 64


alpha_scale = 32.0


def from_everyone(value, axis):
    copies = jnp.broadcast_to(value, (lax.axis_size(axis), *value.shape))
    return lax.all_to_all(copies, axis, split_axis=0, concat_axis=0, tiled=True)


def over_copies(value, axis):
    return from_everyone(value, axis).sum(axis=0)


def cut_along(value, dim, size):
    dims = value.shape
    blocks = value.reshape(*dims[:dim], size, dims[dim] // size, *dims[dim + 1 :])
    return jnp.moveaxis(blocks, dim, 0)


def sum_at_owner(value, axis, dim):
    blocks = cut_along(value, dim, lax.axis_size(axis))
    arrived = lax.all_to_all(blocks, axis, split_axis=0, concat_axis=0, tiled=True)
    return arrived.sum(axis=0)


def in_one_piece(arrays, axis, dim, along):
    both = jnp.concatenate(arrays, axis=along)
    out, at, gathered = (sum_at_owner(both, axis, dim), 0, [])
    for a in arrays:
        gathered.append(lax.slice_in_dim(out, at, at + a.shape[along], axis=along))
        at += a.shape[along]
    return tuple(gathered)


def make_gain(block_tenant_index, ranks, rows, largest_rank):
    tenants = ranks.shape[0]
    rows_tenant = jnp.repeat(block_tenant_index, BLOCK, total_repeat_length=rows)
    columns = jnp.arange(tenants * largest_rank, dtype=jnp.int32)
    col_tenant = columns // largest_rank
    col_slot = columns % largest_rank
    ranks_col = jnp.repeat(ranks, largest_rank, total_repeat_length=tenants * largest_rank)
    keep = (rows_tenant[:, None] == col_tenant[None, :]) & (col_slot[None, :] < ranks_col[None, :])
    scale_col = alpha_scale / ranks_col.astype(jnp.float32)
    return jnp.where(keep, scale_col[None, :], jnp.float32(0.0))


def shards(
    tokens,
    block_tenant_index,
    ranks,
    frozen_up_weight,
    tenant_down_adapters,
    tenant_up_adapters,
    cotangent,
):
    rows = tokens.shape[0]
    local_d = tokens.shape[1]
    local_f = cotangent.shape[1]
    tenants = ranks.shape[0]
    largest_rank = tenant_down_adapters.shape[1]
    gain = make_gain(block_tenant_index, ranks, rows, largest_rank)
    whole = lax.all_gather(tokens, "tenant", axis=1, tiled=True)
    weight = lax.all_gather(frozen_up_weight, ("fsdp", "dp"), axis=0, tiled=True)
    down_part, up_adapter_slice = (
        lax.all_to_all(tenant_down_adapters, "tenant", split_axis=2, concat_axis=0, tiled=True),
        lax.all_to_all(tenant_up_adapters, "tenant", split_axis=2, concat_axis=0, tiled=True),
    )
    local_down = down_part.reshape(tenants * largest_rank, local_d)
    partial_proj = lax.dot_general(
        tokens, local_down, (((1,), (1,)), ((), ())), preferred_element_type=jnp.float32
    )
    proj = lax.psum(partial_proj, "tenant")
    flattened_up = up_adapter_slice.reshape(tenants * largest_rank, local_f)
    adapted = (proj * gain).astype(jnp.bfloat16)
    base = jnp.dot(whole, weight, preferred_element_type=jnp.float32)
    hidden_out = (base + jnp.dot(adapted, flattened_up, preferred_element_type=jnp.float32)).astype(
        jnp.bfloat16
    )
    back_part = lax.dot_general(
        cotangent, flattened_up, (((1,), (1,)), ((), ())), preferred_element_type=jnp.float32
    )
    back = over_copies(back_part, "tenant")
    adapted_grad = (back * gain).astype(jnp.bfloat16)
    base_back = lax.dot_general(
        cotangent, weight, (((1,), (1,)), ((), ())), preferred_element_type=jnp.float32
    )
    grad_base = lax.psum_scatter(base_back, "tenant", scatter_dimension=1, tiled=True)
    grad_tokens = (
        grad_base + jnp.dot(adapted_grad, local_down, preferred_element_type=jnp.float32)
    ).astype(jnp.bfloat16)
    up_term = lax.dot_general(
        adapted, cotangent, (((0,), (0,)), ((), ())), preferred_element_type=jnp.float32
    )
    down_term = lax.dot_general(
        adapted_grad, tokens, (((0,), (0,)), ((), ())), preferred_element_type=jnp.float32
    )
    up_term = up_term.reshape(tenants, largest_rank, local_f)
    down_term = down_term.reshape(tenants, largest_rank, local_d)
    down_share, up_share = in_one_piece((down_term, up_term), "dp", 0, 2)
    grad_down, grad_up = lax.psum((down_share, up_share), "fsdp")
    return (hidden_out, grad_tokens, grad_down, grad_up)


def solution(mesh):
    return jax.shard_map(
        shards,
        mesh=mesh,
        in_specs=(
            P(("fsdp", "dp"), "tenant"),
            P(("fsdp", "dp")),
            P(),
            P(("fsdp", "dp"), "tenant"),
            P("tenant", None, None),
            P("tenant", None, None),
            P(("fsdp", "dp"), "tenant"),
        ),
        out_specs=(
            P(("fsdp", "dp"), "tenant"),
            P(("fsdp", "dp"), "tenant"),
            P("dp", None, "tenant"),
            P("dp", None, "tenant"),
        ),
        check_vma=False,
    )
```

profile of v0, /device:TPU:1, one launch (start us, length us, event | category | flops | bytes accessed | tf_op | source)
XLA Modules:
  0.0 569.7 jit_solution(15425267257277337146)
XLA Ops:
  8.0 0.0 copy-start
  8.0 0.0 all-gather.5.cloned.1.call-start
  8.1 0.7 all-gather.5.cloned.1.call-update
  8.7 0.0 all-reduce.4.cloned.1.call-start
  8.8 6.1 %copy.19 = bf16[1,64,5120]{1,0,2:T(2,128)(2,1)} copy(bf16[1,64,5120]{2,1,0:T(8,128)(2,1)} %param.15) | data formatting | bytes 1310720 | tf_op args[4]
  14.9 0.5 broadcast.409
  15.5 28.9 %reduce.9 = bf16[5120,64]{1,0:T(8,128)(2,1)S(1)} reduce(bf16[5120,1,64]{2,1,0:T(2,128)(2,1)} %bitcast.90, bf16[]{:T(256)} %broadcast.409), dimensions={1}, to_apply=%bitcast.69.reduce_sub_computation | reduce | bytes 1310722
  44.4 0.9 reshape.321
  45.2 20.6 %all_to_all.40 = bf16[8,2,20480]{2,1,0:T(2,128)(2,1)S(1)} all-to-all(bf16[8,2,20480]{2,1,0:T(2,128)(2,1)S(1)} %reshape.321), channel_id=1, replica_groups=mesh['fsdp'=8,'tenant'=8,'dp'=2] {'tenant'}, dimensions={0} | all-to-all | bytes 1310720 | tf_op jit(solution)/shard_map/all_to_all | solution.py:72
  65.9 3.8 reshape.322
  69.6 4.9 copy.20
  74.5 0.0 copy-start.5
  74.5 0.1 copy.25
  74.6 0.1 bitcast_bitcast_fusion.1
  74.7 0.1 copy.21
  74.8 0.8 copy-done.3
  75.6 1.4 fusion.26
  77.0 0.0 all-reduce.4.cloned.1.call-update
  77.0 0.0 all-gather.3.cloned.1.call-start
  77.0 0.7 all-gather.3.cloned.1.call-update
  77.8 0.2 reduce-scatter.2.cloned.1.call-start
  78.0 47.8 %all-gather.5.cloned.1.call-done = bf16[5120,1792]{1,0:T(8,128)(2,1)} async-done(((bf16[320,1792]{1,0:T(8,128)(2,1)}), bf16[5120,1792]{1,0:T(8,128)(2,1)}) %all-gather.5.cloned.1.call-update) | async-done | bytes 18350096 | tf_op jit(solution)/shard_map/all_gather | solution.py:70
  125.8 13.2 %fusion.27 = f32[384,5120]{1,0:T(8,128)} fusion(bf16[384,1792]{1,0:T(8,128)(2,1)S(1)} %copy-done, bf16[5120,1792]{1,0:T(8,128)(2,1)} %all-gather.5.cloned.1.call-done), kind=kOutput, calls=%fused_computation.60 | convolution fusion | flops 7046430720 | bytes 27590656 | tf_op jit(solution)/shard_map/dot_general | solution.py:91
  139.0 0.0 reduce-scatter.2.cloned.1.call-update
  139.0 1.6 copy-done.7
  140.6 11.6 %copy.22 = bf16[1,64,14336]{1,0,2:T(2,128)(2,1)} copy(bf16[1,64,14336]{2,1,0:T(8,128)(2,1)S(1)} %copy-done.7) | data formatting | bytes 3670016 | tf_op args[5]
  152.2 79.7 %reduce.8 = bf16[14336,64]{1,0:T(8,128)(2,1)} reduce(bf16[14336,1,64]{2,1,0:T(2,128)(2,1)} %bitcast.87, bf16[]{:T(256)} %broadcast.409), dimensions={1}, to_apply=%bitcast.67.reduce_sub_computation | reduce | bytes 3670018
  231.9 6.1 %reshape.319 = bf16[8,2,57344]{2,1,0:T(2,128)(2,1)S(1)} reshape(bf16[14336,64]{1,0:T(8,128)(2,1)} %reduce.8) | data formatting | bytes 3670016
  238.0 43.4 %all_to_all.41 = bf16[8,2,57344]{2,1,0:T(2,128)(2,1)} all-to-all(bf16[8,2,57344]{2,1,0:T(2,128)(2,1)S(1)} %reshape.319), channel_id=1, replica_groups=mesh['fsdp'=8,'tenant'=8,'dp'=2] {'tenant'}, dimensions={0} | all-to-all | bytes 3670016 | tf_op jit(solution)/shard_map/all_to_all | solution.py:73
  281.4 7.8 %reshape.320 = bf16[14336,1,64]{2,1,0:T(2,128)(2,1)} reshape(bf16[8,2,57344]{2,1,0:T(2,128)(2,1)} %all_to_all.41) | data formatting | bytes 3670016
  289.2 14.1 %copy.23 = bf16[1,64,14336]{2,1,0:T(8,128)(2,1)S(1)} copy(bf16[1,64,14336]{1,0,2:T(2,128)(2,1)} %bitcast.88) | data formatting | bytes 3670016 | tf_op jit(solution)/shard_map/all_to_all | solution.py:73
  303.3 0.3 copy.28
  303.6 0.1 bitcast_bitcast_fusion
  303.7 0.3 copy.24
  304.0 0.9 fusion.28
  304.9 3.5 broadcast_in_dim.46
  308.5 4.9 all-to-all-start.2
  313.4 0.3 all-reduce.6.cloned.1.call-start
  313.7 0.7 fusion.24
  314.3 0.7 fusion.25
  315.0 0.1 add_add_fusion.1
  315.1 0.1 fusion.8
  315.2 3.7 fusion.16
  318.9 4.4 compare_select_fusion.2
  323.3 0.7 fusion.12
  324.0 0.1 and_select_fusion
  324.1 4.3 fusion.20
  328.4 2.5 fusion.22
  330.9 85.3 %all-to-all-done.2 = f32[8,384,512]{2,1,0:T(8,128)} async-done(((f32[8,384,512]{2,1,0:T(8,128)}), f32[8,384,512]{2,1,0:T(8,128)}, u32[]{:S(2)}, u32[]{:S(2)}) %all-to-all-start.2) | async-done | bytes 6291488 | tf_op jit(solution)/shard_map/all_to_all | solution.py:14
  416.2 3.6 reduce_sum.18
  419.7 0.7 fusion.17
  420.5 2.4 pad_maximum_fusion
  422.9 10.0 %all_to_all.42 = f32[2,4,64,2432]{3,2,1,0:T(8,128)} all-to-all(f32[2,4,64,2432]{3,2,1,0:T(8,128)S(1)} %pad_maximum_fusion), channel_id=1, replica_groups=mesh['fsdp'=8,'tenant'=8,'dp'=2] {'dp'}, dimensions={0} | all-to-all | bytes 9961472 | tf_op jit(solution)/shard_map/all_to_all | solution.py:29
  432.9 4.5 reduce_sum.19
  437.4 2.0 slice.56
  439.3 2.9 slice.57
  442.2 0.0 all-reduce.6.cloned.1.call-update
  442.3 0.0 copy-start.4
  442.3 0.0 all-gather.3.cloned.1.call-done
  442.3 15.8 %fusion = bf16[384,1792]{1,0:T(8,128)(2,1)} fusion(f32[384,1792]{1,0:T(8,128)} %fusion.22, bf16[384,5120]{1,0:T(8,128)(2,1)} %all-gather.3.cloned.1.call-done, bf16[5120,1792]{1,0:T(8,128)(2,1)} %all-gather.5.cloned.1.call-done), kind=kOutput, calls=%fused_computation.2 | convolution fusion | flops 7047806976 | bytes 26411008 | tf_op jit(solution)/shard_map/dot_general | solution.py:82
  458.1 2.5 fusion.1
  460.6 96.5 %all-reduce.6.cloned.1.call-done = (f32[4,64,640]{2,1,0:T(8,128)}, f32[4,64,1792]{2,1,0:T(8,128)}) async-done(((f32[4,64,640]{2,1,0:T(8,128)}, f32[4,64,1792]{2,1,0:T(8,128)}), (f32[4,64,640]{2,1,0:T(8,128)}, f32[4,64,1792]{2,1,0:T(8,128)})) %all-reduce.6.cloned.1.call-update) | async-done | bytes 2490384 | tf_op jit(solution)/shard_map/psum | solution.py:107
  557.2 2.1 copy.34
  559.2 2.9 copy.35
  (26 shorter events, 0.1 us)
Async XLA Ops:
  8.0 117.8 %copy-start = (bf16[384,1792]{1,0:T(8,128)(2,1)S(1)}, bf16[384,1792]{1,0:T(8,128)(2,1)}, u32[]{:S(2)}) copy-start(bf16[384,1792]{1,0:T(8,128)(2,1)} %param.17) | copy-start | bytes 4128772
  8.0 117.8 %all-gather.5.cloned.1.call-start = ((), (), s32[]{:S(2)}) async-start(), calls=%async_computation.6 | async-start | bytes 19496960 | tf_op jit(solution)/shard_map/all_gather | solution.py:70
  8.7 315.3 %all-reduce.4.cloned.1.call-start = ((), (), s32[]{:S(2)}) async-start(), calls=%async_computation.7 | async-start | bytes 1572864 | tf_op jit(solution)/shard_map/psum | solution.py:79
  74.5 1.1 copy-start.5
  74.8 0.8 copy-start.3
  77.0 365.3 %all-gather.3.cloned.1.call-start = ((), (), s32[]{:S(2)}) async-start(), calls=%async_computation.5 | async-start | bytes 4423680 | tf_op jit(solution)/shard_map/all_gather | solution.py:69
  77.8 380.4 %reduce-scatter.2.cloned.1.call-start = ((), (), s32[]{:S(2)}) async-start(), calls=%async_computation.8 | async-start | bytes 8847360 | tf_op jit(solution)/shard_map/reduce_scatter | solution.py:94
  139.0 1.6 copy-start.7
  308.4 5.2 copy-start.9
  308.4 5.9 %copy-start.8 = (s32[8]{0:T(128)S(1)}, s32[8]{0:T(128)}, u32[]{:S(2)}) copy-start(s32[8]{0:T(128)} %param.13) | copy-start | bytes 100
  308.5 6.6 %copy-start.11 = (s32[4,128]{1,0:T(4,128)S(1)}, s32[4,128]{1,0:T(4,128)}, u32[]{:S(2)}) copy-start(s32[4,128]{1,0:T(4,128)} %constant.200.clone.1) | copy-start | bytes 6148
  308.5 6.7 %copy-start.10 = (s32[3,128]{1,0:T(4,128)S(1)}, s32[3,128]{1,0:T(4,128)}, u32[]{:S(2)}) copy-start(s32[3,128]{1,0:T(4,128)} %constant.191.clone.1) | copy-start | bytes 4612
  308.5 107.7 %all-to-all-start.2 = ((f32[8,384,512]{2,1,0:T(8,128)}), f32[8,384,512]{2,1,0:T(8,128)}, u32[]{:S(2)}, u32[]{:S(2)}) async-start(f32[8,384,512]{2,1,0:T(8,128)} %broadcast_in_dim.46), calls=%async_computation.3 | async-start | bytes 12582912 | tf_op jit(solution)/shard_map/all_to_all | solution.py:14
  313.4 243.8 %all-reduce.6.cloned.1.call-start = ((), (), s32[]{:S(2)}) async-start(), calls=%async_computation.9 | async-start | bytes 4980736 | tf_op jit(solution)/shard_map/psum | solution.py:107
  324.1 4.3 copy-start.2
  330.9 88.9 %copy-start.6 = (bf16[384,640]{1,0:T(8,128)(2,1)S(1)}, bf16[384,640]{1,0:T(8,128)(2,1)}, u32[]{:S(2)}) copy-start(bf16[384,640]{1,0:T(8,128)(2,1)} %param.11) | copy-start | bytes 1474564
  442.3 15.9 %copy-start.4 = (bf16[8,1,64,640]{3,2,0,1:T(8,128)(2,1)S(1)}, bf16[8,1,64,640]{3,2,0,1:T(8,128)(2,1)}, u32[]{:S(2)}) copy-start(bf16[8,1,64,640]{3,2,0,1:T(8,128)(2,1)} %copy-done.3) | copy-start | bytes 1966084
  557.2 5.0 copy-start.1
Sparse Core Ops, SparseCore 0:
  10.5 115.2 all-gather.4
  128.1 69.8 all-gather.2
Sparse Core Ops, SparseCore 1:
  77.1 132.6 all-reduce.3
  213.6 200.8 reduce-scatter.1
  442.3 114.8 all-reduce.5
where the time goes:
time: 572 us; the launch traced here: 570 us
  waiting for transfers between devices  231 us (40%)
  other arithmetic  128 us (22%)
  blocking collectives  74 us (13%)
  local copies, waits for them, and re-layouts  73.8 us (13%)
  matrix products  41.3 us (7%)
  between operations  15.9 us (3%)
    unnamed x3, other arithmetic  109 us
    psum x1, waiting for transfers between devices, shards(): grad_down, grad_up = lax.psum((down_share, up_share), 'fsdp')  96.5 us
    all_to_all x1, waiting for transfers between devices, from_everyone(): return lax.all_to_all(copies, axis, split_axis=0, concat_axis=0, tiled=True)  85.3 us
    all_gather x1, waiting for transfers between devices, shards(): lax.all_gather(frozen_up_weight, ('fsdp', 'dp'), axis=0, tiled=True)  47.8 us
    unnamed x35, local copies, waits for them, and re-layouts  44.6 us
    all_to_all x1, blocking collectives, shards(): lax.all_to_all(tenant_up_adapters, 'tenant', split_axis=2, concat_axis=0,...  43.4 us
    all_to_all x1, blocking collectives, shards(): lax.all_to_all(tenant_down_adapters, 'tenant', split_axis=2, concat_axis=...  20.6 us
    dot_general x1, matrix products, shards(): base = jnp.dot(whole, weight, preferred_element_type=jnp.float32)  15.8 us
  transfers between devices with their start and end apart: 6, of which 3 were waited for; matrix products, arithmetic and copies ran while one was open for 41% of the time, Pallas kernels for 0%

commit v1 on v0

v1 whole, which is shorter than its diff:
```python
import jax
import jax.numpy as jnp
from jax import lax
from jax.experimental import pallas as pl
from jax.experimental.pallas import tpu as pltpu
from jax.sharding import PartitionSpec as P

MESH = pl.DeviceIdType.MESH
BF = jnp.bfloat16
F32 = jnp.float32
BLOCK = 64
ALPHA = 32.0
ROUNDS = 5
SUB = 64


def dot(a, b, ca, cb):
    return lax.dot_general(a, b, (((ca,), (cb,)), ((), ())), preferred_element_type=F32)


def kernel(
    bti,
    ranks,
    tokr,
    tok_h,
    w_h,
    dq_h,
    u_h,
    cot_h,
    hid_out,
    gt_out,
    gd_out,
    gu_out,
    tok,
    dq,
    cot,
    wall,
    tokq,
    uall,
    hacc,
    gsend,
    gown,
    grecv,
    gzs,
    gzr,
    gcomp,
    cp2,
    brecv,
    agx,
    agj,
    agexp,
    asend,
    arecv,
    aexp,
    gpart,
    gpr,
    rss,
    rsr,
    agg,
    lsem,
    wss,
    wrs,
    prs,
    tss,
    trs,
    uss,
    urs,
    upss,
    uprs,
    bss,
    brs,
    ass_,
    ars,
    dss,
    drs,
    gss,
    grs,
    zss,
    zrs,
    xss,
    xrs,
    rss_s,
    rss_r,
    ags_s,
    ags_r,
):
    f = lax.axis_index("fsdp")
    j = lax.axis_index("tenant")
    c = lax.axis_index("dp")
    rows = cot.shape[0]
    half = rows // 2
    lf = cot.shape[1]

    def ring(i):
        flip = 1 - 2 * lax.rem(i, 2)
        right, left, opp = lax.rem(i + 2, 8), lax.rem(i + 6, 8), lax.rem(i + 4, 8)
        return dict(
            Z=i + flip,
            R=right,
            L=left,
            O=opp,
            RZ=right + flip,
            LZ=left + flip,
            OZ=opp + flip,
        )

    fn, tn = ring(f), ring(j)
    y, zh = j // 2, lax.rem(j, 2)
    partner = {"dp": 1 - c}

    def rc(src, dst, ss, rs, dev):
        return pltpu.make_async_remote_copy(
            src_ref=src, dst_ref=dst, send_sem=ss, recv_sem=rs, device_id=dev, device_id_type=MESH
        )

    def each(lo, hi, body):
        def step(k, carry):
            body(k)
            return carry

        lax.fori_loop(lo, hi, step, 0)

    sent = []

    def go(src, dst, ss, rs, dev):
        d = rc(src, dst, ss, rs, dev)
        d.start()
        sent.append(d)

    def got(dst, rs):
        rc(dst, dst, rs, rs, partner).wait_recv()

    def slot(q, fi, ci):
        return wall.at[q, pl.ds((2 * fi + ci) * SUB, SUB)]

    def part(q, fi, ci, h):
        return wall.at[q, pl.ds((2 * fi + ci) * SUB + h * (SUB // 2), SUB // 2)]

    wloc = [
        pltpu.make_async_copy(w_h.at[pl.ds(q * SUB, SUB)], slot(q, f, c), lsem.at[q])
        for q in range(ROUNDS)
    ]
    tloc = pltpu.make_async_copy(tokr, tokq.at[j], lsem.at[5])
    uloc = pltpu.make_async_copy(
        u_h.at[:, pl.ds(pl.multiple_of(j * lf, 128), lf)], uall.at[j], lsem.at[6]
    )
    cloc = pltpu.make_async_copy(cot_h, cot, lsem.at[7])
    dloc = pltpu.make_async_copy(dq_h, dq, lsem.at[8])
    kloc = pltpu.make_async_copy(tok_h, tok, lsem.at[9])
    for d in [*wloc, tloc, uloc, cloc, dloc, kloc]:
        d.start()

    barrier = pltpu.get_barrier_semaphore()
    for k in range(1, 8):
        pl.semaphore_signal(barrier, 1, device_id={"fsdp": lax.rem(f + k, 8)}, device_id_type=MESH)
        pl.semaphore_signal(
            barrier, 1, device_id={"tenant": lax.rem(j + k, 8)}, device_id_type=MESH
        )
    pl.semaphore_signal(barrier, 1, device_id=partner, device_id_type=MESH)
    pl.semaphore_wait(barrier, 15)

    def fs(i):
        return {"fsdp": fn[i]}

    def w_send(q, name, i, rsem, to, src=None):
        ref = slot(q, fn[name] if name else f, c) if src is None else src
        go(ref, ref, wss.at[q, i], rsem, to)

    def w_got(q, k, ref):
        got(ref, wrs.at[q, k])

    def w_A(q):
        wloc[q].wait()
        w_send(q, None, 0, wrs.at[q, 1], fs("R"))
        w_send(q, None, 1, wrs.at[q, 2], fs("L"))
        w_send(q, None, 2, wrs.at[q, 0], fs("Z"))
        w_send(q, None, 3, prs.at[q, 0], partner)

    def w_B(q):
        w_got(q, 0, slot(q, fn["Z"], c))
        w_send(q, "Z", 4, wrs.at[q, 3], fs("R"))
        w_send(q, "Z", 5, wrs.at[q, 4], fs("L"))
        w_send(q, "Z", 6, prs.at[q, 1], partner)

    def w_CD(q, left, right, kl, kr, kt, kb, i, p):
        w_got(q, kl, slot(q, fn[left], c))
        w_send(q, left, i, wrs.at[q, kt], fs("R"), part(q, fn[left], c, 0))
        w_send(q, left, i + 1, prs.at[q, p], partner)
        w_got(q, kr, slot(q, fn[right], c))
        w_send(q, right, i + 2, wrs.at[q, kb], fs("L"), part(q, fn[right], c, 1))
        w_send(q, right, i + 3, prs.at[q, p + 1], partner)

    def w_C(q):
        w_CD(q, "L", "R", 1, 2, 5, 6, 7, 2)

    def w_D(q):
        w_CD(q, "LZ", "RZ", 3, 4, 7, 8, 11, 4)

    def w_E(q):
        for name, k, i, p in (("O", 5, 15, 6), ("OZ", 7, 16, 7)):
            w_got(q, k, part(q, fn[name], c, 0))
            w_got(q, k + 1, part(q, fn[name], c, 1))
            w_send(q, name, i, prs.at[q, p], partner)

    def w_P(q):
        for p, name in enumerate((None, "Z", "L", "R", "LZ", "RZ", "O", "OZ")):
            got(slot(q, fn[name] if name else f, 1 - c), prs.at[q, p])

    def te(i):
        return {"tenant": tn[i]}

    def t_send(ji, i, k, to, h=None):
        ref = tokq.at[ji] if h is None else tokq.at[ji, :, pl.ds(h * half, half)]
        go(ref, ref, tss.at[i], trs.at[k], to)

    def t_A():
        tloc.wait()
        t_send(j, 2, 0, te("Z"))
        t_send(j, 0, 1, te("R"))
        t_send(j, 1, 2, te("L"))

    def t_B():
        got(tokq.at[tn["Z"]], trs.at[0])
        t_send(tn["Z"], 3, 3, te("R"))
        t_send(tn["Z"], 4, 4, te("L"))

    def t_CD(left, right, kl, kr, kt, kb, i):
        got(tokq.at[tn[left]], trs.at[kl])
        t_send(tn[left], i, kt, te("R"), 0)
        got(tokq.at[tn[right]], trs.at[kr])
        t_send(tn[right], i + 1, kb, te("L"), 1)

    def t_E():
        for name, k in (("O", 5), ("OZ", 7)):
            for h in range(2):
                got(tokq.at[tn[name], :, pl.ds(h * half, half)], trs.at[k + h])

    def u_half(ji, ci):
        return uall.at[ji, pl.ds(ci * 32, 32)]

    def u_desc(k):
        to = lax.rem(j + k, 8)
        return rc(
            u_h.at[pl.ds(c * 32, 32), pl.ds(pl.multiple_of(to * lf, 128), lf)],
            u_half(j, c),
            uss.at[k],
            urs.at[k],
            {"tenant": to},
        )

    def up_desc(k):
        ref = u_half(lax.rem(j + 8 - k, 8), c)
        return rc(ref, ref, upss.at[k], uprs.at[k], partner)

    def u_recv(k):
        got(u_half(lax.rem(j + 8 - k, 8), c), urs.at[k])
        up_desc(k).start()

    def tenant_is(b, t, shape):
        return jnp.full(shape, bti[b], jnp.int32) == t

    def make_gain():
        lane = lax.broadcasted_iota(jnp.int32, (BLOCK, BLOCK), 1)
        gains = []
        for t in range(8):
            r = jnp.full((BLOCK, BLOCK), ranks[t], jnp.int32)
            gains.append(jnp.where(lane < r, ALPHA / r.astype(F32), 0.0))
        for b in range(6):
            g = jnp.zeros((BLOCK, BLOCK), F32)
            for t in range(8):
                g = jnp.where(tenant_is(b, t, g.shape), gains[t], g)
            gcomp[pl.ds(b * BLOCK, BLOCK), :] = g

    def back_part():
        for h in range(2):
            u = uall[pl.ds(4 * h, 4)].reshape(256, lf)
            p = dot(cot[...], u, 1, 1)
            for b in range(6):
                rs = slice(b * BLOCK, (b + 1) * BLOCK)
                acc = jnp.zeros((BLOCK, BLOCK), F32)
                for t in range(4):
                    acc = jnp.where(
                        tenant_is(b, 4 * h + t, acc.shape), p[rs, 64 * t : 64 * t + 64], acc
                    )
                at = (slice(rs.start % half, rs.start % half + BLOCK), slice(64 * (b // 3), 64 * (b // 3) + 64))
                cp2[at] = acc if h == 0 else cp2[at] + acc

    def b_desc(k):
        to = lax.rem(j + k, 8)
        return rc(cp2.at[pl.ds(to * 24, 24)], brecv.at[k], bss.at[k], brs.at[k], {"tenant": to})

    def b_sum():
        s = cp2[pl.ds(pl.multiple_of(j * 24, 8), 24), :]
        for k in range(1, 8):
            got(brecv.at[k], brs.at[k])
            s = s + brecv[k]
        agx[j] = s

    def ag_desc(k):
        return rc(agx.at[j], agx.at[j], ass_.at[k], ars.at[k], {"tenant": lax.rem(j + k, 8)})

    def ag_use():
        for k in range(1, 8):
            got(agx.at[lax.rem(j + 8 - k, 8)], ars.at[k])
        packed = jnp.concatenate([agx[k] for k in range(8)], axis=0)
        for b in range(6):
            r0 = (b % 3) * BLOCK
            s = packed[r0 : r0 + BLOCK, 64 * (b // 3) : 64 * (b // 3) + 64]
            v = (s * gcomp[b * BLOCK : (b + 1) * BLOCK, :]).astype(BF).astype(F32)
            zero = jnp.zeros_like(v)
            rs = slice(b * BLOCK, (b + 1) * BLOCK)
            agj[rs, :] = jnp.where(tenant_is(b, j, v.shape), v, zero).astype(BF)
            for t in range(0, 8, 2):
                pair = jnp.concatenate(
                    [jnp.where(tenant_is(b, t + e, v.shape), v, zero) for e in range(2)], axis=1
                )
                agexp[rs, 64 * t : 64 * t + 128] = pair.astype(BF)

    def lhs(q):
        return jnp.concatenate([tokq[i, q] for i in range(8)], axis=1)

    def adapted_part():
        p = dot(lhs(0), dq[0], 1, 1)
        for q in range(1, ROUNDS):
            p = p + dot(lhs(q), dq[q], 1, 1)
        outs = []
        for b in range(6):
            rs = slice(b * BLOCK, (b + 1) * BLOCK)
            v = p[rs] * gcomp[rs, :]
            outs.append(jnp.where(tenant_is(b, j, v.shape), v, jnp.zeros_like(v)))
        for b in range(3):
            pair = jnp.concatenate([outs[b], outs[b + 3]], axis=1).astype(BF)
            asend[b * BLOCK : (b + 1) * BLOCK, :] = pair
            arecv[j, pl.ds(b * BLOCK, BLOCK), :] = pair

    def d_desc(k):
        return rc(asend, arecv.at[j], dss.at[k], drs.at[k], {"tenant": lax.rem(j + k, 8)})

    def adapted_use():
        for k in range(1, 8):
            got(arecv.at[lax.rem(j + 8 - k, 8)], drs.at[k])
        for t in range(0, 8, 2):
            a0, a1 = arecv[t], arecv[t + 1]
            aexp[:half, 64 * t : 64 * t + 128] = jnp.concatenate([a0[:, :64], a1[:, :64]], axis=1)
            aexp[half:, 64 * t : 64 * t + 128] = jnp.concatenate([a0[:, 64:], a1[:, 64:]], axis=1)

    def grad_down_part():
        p = dot(agexp[...], tok[...], 0, 0)
        gpart[0, :, 0:640] = p[:256]
        gpart[1, :, 0:640] = p[256:]

    def grad_up_part():
        def body(n):
            at = pl.ds(pl.multiple_of(n * 256, 256), 256)
            to = pl.ds(pl.multiple_of(640 + n * 256, 128), 256)
            p = dot(aexp[...], cot[:, at], 0, 0)
            gpart[0, :, to] = p[:256]
            gpart[1, :, to] = p[256:]

        each(0, lf // 256, body)

    def rs_make():
        got(gpr, xrs)

        def body(k):
            at = pl.ds(pl.multiple_of(k * 32, 32), 32)
            rss[k] = (gpart[c, at, :] + gpr[at, :]).astype(BF)

        each(0, 8, body)

    def rs_desc(k):
        to = lax.rem(f + k, 8)
        return rc(rss.at[to], rsr.at[k], rss_s.at[k], rss_r.at[k], {"fsdp": to})

    def rs_sum():
        at = pl.ds(pl.multiple_of(f * 32, 32), 32)
        for k in range(1, 8):
            got(rsr.at[k], rss_r.at[k])
        s = gpart[c, at, :] + gpr[at, :]
        for k in range(1, 8):
            s = s + rsr[k].astype(F32)
        agg[f] = s.astype(BF)

    def gg_desc(k):
        return rc(agg.at[f], agg.at[f], ags_s.at[k], ags_r.at[k], {"fsdp": lax.rem(f + k, 8)})

    def grads_out():
        for k in range(1, 8):
            got(agg.at[lax.rem(f + 8 - k, 8)], ags_r.at[k])

        def body(k):
            at = pl.ds(pl.multiple_of(k * 32, 32), 32)
            v = agg[k].astype(F32)
            gd_out[at, :] = v[:, :640]
            gu_out[at, :] = v[:, 640:]

        each(0, 8, body)

    def g_desc(q, i):
        rel = lax.rem(y - i + 4, 4) - 1
        return rc(
            gsend.at[q, i], grecv.at[q, rel], gss.at[q, i], grs.at[q, rel], {"tenant": 2 * i + zh}
        )

    def compute_g(q):
        def body(k):
            i = lax.rem(y + k, 4)
            at = pl.ds(pl.multiple_of(i * 256, 256), 256)
            p = dot(cot[...], wall[q, at, :], 1, 1) + dot(agj[...], dq[q, :, at], 1, 0)

            @pl.when(k < 4)
            def _():
                gsend[q, i] = p.astype(BF)
                g_desc(q, i).start()

            @pl.when(k == 4)
            def _():
                gown[q] = p

        each(1, 5, body)

    def compute_h(q):
        def body(n):
            at = pl.ds(pl.multiple_of(n * 256, 256), 256)
            p = dot(lhs(q), wall[q, :, at], 1, 0)
            if q == 0:
                hacc[:, at] = p
            elif q < ROUNDS - 1:
                hacc[:, at] += p
            else:
                u = uall[:, :, at].reshape(512, 256)
                hid_out[:, at] = (hacc[:, at] + p + dot(aexp[...], u, 1, 0)).astype(BF)

        each(0, lf // 256, body)

    def compute(q):
        w_P(q)
        compute_g(q)
        compute_h(q)

    def g_sum(q):
        for k in range(3):
            got(grecv.at[q, k], grs.at[q, k])
        mine = pl.ds(pl.multiple_of(zh * 128, 128), 128)
        other = pl.ds(pl.multiple_of(128 - zh * 128, 128), 128)

        def total(at):
            s = gown[q, :, at]
            for k in range(3):
                s = s + grecv[q, k, :, at].astype(F32)
            return s

        gzs[q] = total(other).astype(BF)
        go(gzs.at[q], gzr.at[q], zss.at[q], zrs.at[q], te("Z"))
        gown[q, :, mine] = total(mine)

    def gt_final():
        mine = pl.ds(pl.multiple_of(zh * 128, 128), 128)
        for q in range(ROUNDS):
            got(gzr.at[q], zrs.at[q])

        def body(b):
            at = pl.ds(pl.multiple_of(b * BLOCK, BLOCK), BLOCK)
            s = [gown[q, at, mine] + gzr[q, at, :].astype(F32) for q in range(ROUNDS)]
            row = jnp.concatenate([v[:, :64] for v in s] + [v[:, 64:] for v in s], axis=1)
            gt_out[at, :] = row.astype(BF)

        each(0, 6, body)

    w_A(0)
    w_A(1)
    each(1, 8, lambda k: u_desc(k).start())
    t_A()
    make_gain()

    w_B(0)
    w_C(0)
    w_A(2)
    t_B()
    w_D(0)

    w_B(1)
    w_C(1)
    w_A(3)
    each(1, 8, u_recv)
    t_CD("L", "R", 1, 2, 5, 6, 5)
    w_D(1)
    w_E(0)
    uloc.wait()
    cloc.wait()
    each(1, 8, lambda k: got(u_half(lax.rem(j + 8 - k, 8), 1 - c), uprs.at[k]))
    back_part()
    each(1, 8, lambda k: b_desc(k).start())

    w_B(2)
    w_C(2)
    w_A(4)
    b_sum()
    each(1, 8, lambda k: ag_desc(k).start())
    t_CD("LZ", "RZ", 3, 4, 7, 8, 7)
    w_D(2)
    w_E(1)
    ag_use()
    kloc.wait()
    grad_down_part()
    t_E()
    dloc.wait()
    adapted_part()
    each(1, 8, lambda k: d_desc(k).start())
    compute(0)

    w_B(3)
    w_C(3)
    w_D(3)
    w_E(2)
    adapted_use()
    grad_up_part()
    go(gpart.at[1 - c], gpr, xss, xrs, partner)
    compute(1)

    w_B(4)
    w_C(4)
    rs_make()
    each(1, 8, lambda k: rs_desc(k).start())
    w_D(4)
    w_E(3)
    compute(2)
    g_sum(0)
    compute(3)
    g_sum(1)

    w_E(4)
    rs_sum()
    each(1, 8, lambda k: gg_desc(k).start())
    g_sum(2)
    compute(4)
    g_sum(3)
    g_sum(4)
    grads_out()
    gt_final()

    for d in sent:
        d.wait_send()
    each(1, 8, lambda k: u_desc(k).wait_send())
    each(1, 8, lambda k: up_desc(k).wait_send())
    each(1, 8, lambda k: b_desc(k).wait_send())
    each(1, 8, lambda k: ag_desc(k).wait_send())
    each(1, 8, lambda k: d_desc(k).wait_send())
    each(1, 8, lambda k: rs_desc(k).wait_send())
    each(1, 8, lambda k: gg_desc(k).wait_send())
    for q in range(ROUNDS):
        each(1, 4, lambda k: g_desc(q, lax.rem(y + k, 4)).wait_send())


def shards(tokens, bti, ranks, w, down, up, cot):
    rows, ld = tokens.shape
    lf = cot.shape[1]
    d = down.shape[2]
    tokr = tokens.reshape(rows, 2, ROUNDS, SUB).transpose(2, 0, 1, 3).reshape(ROUNDS, rows, 128)
    dq = down.reshape(64, 8, 2, ROUNDS, SUB).transpose(3, 0, 1, 2, 4).reshape(ROUNDS, 64, 1024)
    up = up.reshape(64, up.shape[2])
    dma = pltpu.SemaphoreType.DMA
    vm = pltpu.VMEM
    smem = pl.BlockSpec(memory_space=pltpu.SMEM)
    hbm = pl.BlockSpec(memory_space=pl.ANY)
    out = pl.BlockSpec(memory_space=pltpu.VMEM)
    half = rows // 2
    hid, gt, gd, gu = pl.pallas_call(
        kernel,
        out_shape=(
            jax.ShapeDtypeStruct((rows, lf), BF),
            jax.ShapeDtypeStruct((rows, ld), BF),
            jax.ShapeDtypeStruct((256, ld), F32),
            jax.ShapeDtypeStruct((256, lf), F32),
        ),
        in_specs=[smem, smem, hbm, hbm, hbm, hbm, hbm, hbm],
        out_specs=(out, out, out, out),
        scratch_shapes=[
            vm((rows, ld), BF),
            vm((ROUNDS, 64, 1024), BF),
            vm((rows, lf), BF),
            vm((ROUNDS, 1024, lf), BF),
            vm((8, ROUNDS, rows, 128), BF),
            vm((8, 64, lf), BF),
            vm((rows, lf), F32),
            vm((ROUNDS, 4, rows, 256), BF),
            vm((ROUNDS, rows, 256), F32),
            vm((ROUNDS, 3, rows, 256), BF),
            vm((ROUNDS, rows, 128), BF),
            vm((ROUNDS, rows, 128), BF),
            vm((rows, 64), F32),
            vm((half, 128), F32),
            vm((8, 24, 128), F32),
            vm((8, 24, 128), F32),
            vm((rows, 64), BF),
            vm((rows, 512), BF),
            vm((half, 128), BF),
            vm((8, half, 128), BF),
            vm((rows, 512), BF),
            vm((2, 256, ld + lf), F32),
            vm((256, ld + lf), F32),
            vm((8, 32, ld + lf), BF),
            vm((8, 32, ld + lf), BF),
            vm((8, 32, ld + lf), BF),
            dma((10,)),
            dma((ROUNDS, 17)),
            dma((ROUNDS, 9)),
            dma((ROUNDS, 8)),
            dma((9,)),
            dma((9,)),
            dma((8,)),
            dma((8,)),
            dma((8,)),
            dma((8,)),
            dma((8,)),
            dma((8,)),
            dma((8,)),
            dma((8,)),
            dma((8,)),
            dma((8,)),
            dma((ROUNDS, 4)),
            dma((ROUNDS, 3)),
            dma((ROUNDS,)),
            dma((ROUNDS,)),
            dma,
            dma,
            dma((8,)),
            dma((8,)),
            dma((8,)),
            dma((8,)),
        ],
        compiler_params=pltpu.CompilerParams(
            collective_id=0, has_side_effects=True, vmem_limit_bytes=67043328
        ),
    )(bti, ranks, tokr, tokens, w, dq, up, cot)
    return hid, gt, gd.reshape(4, 64, ld), gu.reshape(4, 64, lf)


def solution(mesh):
    return jax.shard_map(
        shards,
        mesh=mesh,
        in_specs=(
            P(("fsdp", "dp"), "tenant"),
            P(("fsdp", "dp")),
            P(),
            P(("fsdp", "dp"), "tenant"),
            P("tenant", None, None),
            P("tenant", None, None),
            P(("fsdp", "dp"), "tenant"),
        ),
        out_specs=(
            P(("fsdp", "dp"), "tenant"),
            P(("fsdp", "dp"), "tenant"),
            P("dp", None, "tenant"),
            P("dp", None, "tenant"),
        ),
        check_vma=False,
    )
```

time: 572 us -> 155 us (0.27)
  waiting for transfers between devices: 231 us -> 0 us
  Pallas kernels: 0 us -> 142 us
  other arithmetic: 128 us -> 0 us
  blocking collectives: 74 us -> 0 us
  local copies, waits for them, and re-layouts: 73.8 us -> 11.7 us
  matrix products: 41.3 us -> 0 us
  between operations: 15.9 us -> 0.69 us
    pallas_call x0 -> x1, Pallas kernels: none -> 142 us  [shards(): pl.pallas_call(kernel, out_shape=(jax.ShapeDtypeStruct((rows, lf), BF), j...]
    unnamed x3 -> x0, other arithmetic: 109 us -> none
    psum x2 -> x0, waiting for transfers between devices: 96.5 us -> none  [the longest x1 96.5 us: shards(): grad_down, grad_up = lax.psum((down_share, up_share), 'fsdp')]
    all_to_all x1 -> x0, waiting for transfers between devices: 85.3 us -> none  [from_everyone(): return lax.all_to_all(copies, axis, split_axis=0, concat_axis=0, tiled=True)]
    all_to_all x3 -> x0, blocking collectives: 74 us -> none  [the longest x1 43.4 us: shards(): lax.all_to_all(tenant_up_adapters, 'tenant', split_axis=2, concat_axis=0,...]
    all_gather x2 -> x0, waiting for transfers between devices: 47.8 us -> none  [the longest x1 47.8 us: shards(): lax.all_gather(frozen_up_weight, ('fsdp', 'dp'), axis=0, tiled=True)]
    dot_general x8 -> x0, matrix products: 41.3 us -> none  [the longest x1 15.8 us: shards(): base = jnp.dot(whole, weight, preferred_element_type=jnp.float32)]
    unnamed x35 -> x14, local copies, waits for them, and re-layouts: 44.6 us -> 7.6 us
  transfers between devices with their start and end apart: 6 -> 0, of which waited for: 3 -> 0; matrix products, arithmetic and copies ran while one was open for 41% -> 0% of each run, Pallas kernels for 0% -> 0%
where the time goes in v1:
time: 155 us; the launch traced here: 154 us
  Pallas kernels  142 us (92%)
  local copies, waits for them, and re-layouts  11.7 us (8%)
    pallas_call x1, Pallas kernels, shards(): pl.pallas_call(kernel, out_shape=(jax.ShapeDtypeStruct((rows, lf), BF), j...  142 us
    unnamed x14, local copies, waits for them, and re-layouts  7.6 us

profile of v1, /device:TPU:1, one launch (start us, length us, event | category | flops | bytes accessed | tf_op | source)
XLA Modules:
  0.0 154.4 jit_solution(11559736450417253427)
XLA Ops:
  0.6 0.0 copy-start.2
  0.6 1.4 copy.13
  2.0 0.1 copy.14
  2.1 1.0 copy.17.tokr
  3.1 0.0 copy-done.2
  3.1 0.7 copy.15
  3.8 1.3 copy.16
  5.1 1.7 %reshape.32.dq_h = bf16[5,64,1024]{2,1,0:T(8,128)(2,1)} reshape(bf16[5,64,8,2,64]{4,3,2,1,0:T(2,128)(2,1)S(1)} %copy.16) | data formatting | bytes 1310720 | tf_op jit(solution)/shard_map/reshape | solution.py:560
  6.8 142.0 %shard_map.102 = (bf16[384,1792]{1,0:T(8,128)(2,1)}, bf16[384,640]{1,0:T(8,128)(2,1)}, f32[256,640]{1,0:T(8,128)}, f32[256,1792]{1,0:T(8,128)}) custom-call(s32[6]{0:T(128)} %bti.1, s32[8]{0:T(128)} %ranks.1, bf16[5,384,128]{2,1,0:T(8,128)(2,1)} %copy.17.tokr, bf16[384,640]{1,0:T(8,128)(2,1)} %tok_h.1, bf16[320,1792]{1,0:T(8,128)(2,1)} %w_h.1, ...), custom_call_target="tpu_custom_call" | custom-call | tf_op jit(solution)/shard_map/pallas_call | solution.py:568
  148.8 0.0 copy-start.3
  148.8 0.0 copy-start.1
  148.8 2.6 %copy.22 = bf16[384,1792]{1,0:T(8,128)(2,1)} copy(bf16[384,1792]{1,0:T(8,128)(2,1)} %get-tuple-element.16) | data formatting | bytes 2752512
  151.4 0.0 copy-done.3
  151.4 0.0 copy-start
  151.4 0.8 copy.23
  152.2 0.0 copy-done.1
  152.2 0.8 copy.24
  153.1 0.1 copy-done
  153.1 1.2 copy.25
Async XLA Ops:
  0.6 2.4 %copy-start.2 = (bf16[1,64,5120]{2,1,0:T(8,128)(2,1)S(1)}, bf16[1,64,5120]{2,1,0:T(8,128)(2,1)}, u32[]{:S(2)}) copy-start(bf16[1,64,5120]{2,1,0:T(8,128)(2,1)} %param.11) | copy-start | bytes 1966084
  148.8 2.6 %copy-start.3 = (bf16[384,640]{1,0:T(8,128)(2,1)S(1)}, bf16[384,640]{1,0:T(8,128)(2,1)}, u32[]{:S(2)}) copy-start(bf16[384,640]{1,0:T(8,128)(2,1)} %get-tuple-element.17) | copy-start | bytes 1474564
  148.8 3.4 %copy-start.1 = (f32[256,640]{1,0:T(8,128)S(1)}, f32[256,640]{1,0:T(8,128)}, u32[]{:S(2)}) copy-start(f32[256,640]{1,0:T(8,128)} %get-tuple-element.10) | copy-start | bytes 1966084
  151.4 1.7 %copy-start = (f32[256,1792]{1,0:T(8,128)S(1)}, f32[256,1792]{1,0:T(8,128)}, u32[]{:S(2)}) copy-start(f32[256,1792]{1,0:T(8,128)} %get-tuple-element.11) | copy-start | bytes 5505028

commit v2 on v1

--- a/solution.py
+++ b/solution.py
@@ -21,10 +21,9 @@
 def kernel(
     bti,
     ranks,
-    tokr,
     tok_h,
     w_h,
-    dq_h,
+    d_h,
     u_h,
     cot_h,
     hid_out,
@@ -36,7 +35,11 @@
     cot,
     wall,
     tokq,
+    dmine,
     uall,
+    dall,
+    ux,
+    dx,
     hacc,
     gsend,
     gown,
@@ -49,8 +52,6 @@
     agx,
     agj,
     agexp,
-    asend,
-    arecv,
     aexp,
     gpart,
     gpr,
@@ -71,8 +72,6 @@
     brs,
     ass_,
     ars,
-    dss,
-    drs,
     gss,
     grs,
     zss,
@@ -89,7 +88,7 @@
     c = lax.axis_index("dp")
     rows = cot.shape[0]
     half = rows // 2
-    lf = cot.shape[1]
+    lf, ld = cot.shape[1], tok.shape[1]
 
     def ring(i):
         flip = 1 - 2 * lax.rem(i, 2)
@@ -140,14 +139,14 @@
         pltpu.make_async_copy(w_h.at[pl.ds(q * SUB, SUB)], slot(q, f, c), lsem.at[q])
         for q in range(ROUNDS)
     ]
-    tloc = pltpu.make_async_copy(tokr, tokq.at[j], lsem.at[5])
-    uloc = pltpu.make_async_copy(
-        u_h.at[:, pl.ds(pl.multiple_of(j * lf, 128), lf)], uall.at[j], lsem.at[6]
-    )
-    cloc = pltpu.make_async_copy(cot_h, cot, lsem.at[7])
-    dloc = pltpu.make_async_copy(dq_h, dq, lsem.at[8])
-    kloc = pltpu.make_async_copy(tok_h, tok, lsem.at[9])
-    for d in [*wloc, tloc, uloc, cloc, dloc, kloc]:
+    ucol = pl.ds(pl.multiple_of(j * lf, 128), lf)
+    dcol = pl.ds(pl.multiple_of(j * ld, 128), ld)
+    kloc = pltpu.make_async_copy(tok_h, tok, lsem.at[5])
+    mloc = pltpu.make_async_copy(d_h, dmine, lsem.at[6])
+    uloc = pltpu.make_async_copy(u_h.at[:, ucol], uall.at[j], lsem.at[7])
+    dloc = pltpu.make_async_copy(d_h.at[:, dcol], dall.at[j], lsem.at[8])
+    cloc = pltpu.make_async_copy(cot_h, cot, lsem.at[9])
+    for d in [*wloc, kloc, mloc, uloc, dloc, cloc]:
         d.start()
 
     barrier = pltpu.get_barrier_semaphore()
@@ -157,7 +156,10 @@
             barrier, 1, device_id={"tenant": lax.rem(j + k, 8)}, device_id_type=MESH
         )
     pl.semaphore_signal(barrier, 1, device_id=partner, device_id_type=MESH)
-    pl.semaphore_wait(barrier, 15)
+    pl.semaphore_signal(
+        barrier, 1, device_id={"fsdp": fn["Z"], "tenant": tn["Z"]}, device_id_type=MESH
+    )
+    pl.semaphore_wait(barrier, 16)
 
     def fs(i):
         return {"fsdp": fn[i]}
@@ -213,11 +215,29 @@
         ref = tokq.at[ji] if h is None else tokq.at[ji, :, pl.ds(h * half, half)]
         go(ref, ref, tss.at[i], trs.at[k], to)
 
+    def pieces(v):
+        return [
+            jnp.concatenate([v[:, SUB * q : SUB * q + SUB], v[:, 320 + SUB * q : 384 + SUB * q]], axis=1)
+            for q in range(ROUNDS)
+        ]
+
+    def t_make():
+        kloc.wait()
+        for q, v in enumerate(pieces(tok[...])):
+            tokq[j, q] = v
+
+    def dq_make():
+        mloc.wait()
+        for i in range(8):
+            for q, v in enumerate(pieces(dmine[:, ld * i : ld * i + ld])):
+                dq[q, :, 128 * i : 128 * i + 128] = v
+
     def t_A():
-        tloc.wait()
-        t_send(j, 2, 0, te("Z"))
         t_send(j, 0, 1, te("R"))
         t_send(j, 1, 2, te("L"))
+
+    def t_Z():
+        t_send(j, 2, 0, te("Z"))
 
     def t_B():
         got(tokq.at[tn["Z"]], trs.at[0])
@@ -230,31 +250,68 @@
         got(tokq.at[tn[right]], trs.at[kr])
         t_send(tn[right], i + 1, kb, te("L"), 1)
 
+    def t_C():
+        t_CD("L", "R", 1, 2, 5, 6, 5)
+
+    def t_D():
+        t_CD("LZ", "RZ", 3, 4, 7, 8, 7)
+
     def t_E():
         for name, k in (("O", 5), ("OZ", 7)):
             for h in range(2):
                 got(tokq.at[tn[name], :, pl.ds(h * half, half)], trs.at[k + h])
 
-    def u_half(ji, ci):
-        return uall.at[ji, pl.ds(ci * 32, 32)]
-
-    def u_desc(k):
-        to = lax.rem(j + k, 8)
-        return rc(
-            u_h.at[pl.ds(c * 32, 32), pl.ds(pl.multiple_of(to * lf, 128), lf)],
-            u_half(j, c),
-            uss.at[k],
-            urs.at[k],
-            {"tenant": to},
-        )
-
-    def up_desc(k):
-        ref = u_half(lax.rem(j + 8 - k, 8), c)
-        return rc(ref, ref, upss.at[k], uprs.at[k], partner)
-
-    def u_recv(k):
-        got(u_half(lax.rem(j + 8 - k, 8), c), urs.at[k])
-        up_desc(k).start()
+    def adapter(src, width, all_, relay, s):
+        def own(ji, ci):
+            return all_.at[ji, pl.ds(ci * 32, 32)]
+
+        def out(ji):
+            return src.at[pl.ds(c * 32, 32), pl.ds(pl.multiple_of(ji * width, 128), width)]
+
+        return own, out, relay, s
+
+    kinds = (adapter(d_h, ld, dall, dx, 0), adapter(u_h, lf, uall, ux, 10))
+    cross = {"fsdp": fn["Z"], "tenant": tn["Z"]}
+
+    def at_y(r):
+        return lax.rem(y + r, 4)
+
+    def u_cross():
+        for own, out, relay, s in kinds:
+            for r in range(4):
+                dst = own(j, c) if r == 0 else relay.at[r]
+                go(out(2 * at_y(r) + 1 - zh), dst, uss.at[s + r], urs.at[s + r], cross)
+
+    def u_own():
+        for own, out, relay, s in kinds:
+            for r in range(1, 4):
+                to, k = 2 * at_y(r) + zh, s + 3 + r
+                go(out(to), own(j, c), uss.at[k], urs.at[k], {"tenant": to})
+
+    def u_fwd():
+        for own, out, relay, s in kinds:
+            for r in range(1, 4):
+                got(relay.at[r], urs.at[s + r])
+                to, k = 2 * at_y(r) + zh, s + 6 + r
+                go(relay.at[r], own(tn["Z"], c), uss.at[k], urs.at[k], {"tenant": to})
+
+    def u_slots(s):
+        yield tn["Z"], s, s
+        for r in range(1, 4):
+            yield 2 * at_y(4 - r) + zh, s + 3 + r, s + r
+        for r in range(1, 4):
+            yield 2 * at_y(4 - r) + 1 - zh, s + 6 + r, s + 3 + r
+
+    def u_recv():
+        for own, out, relay, s in kinds:
+            for ji, k, p in u_slots(s):
+                got(own(ji, c), urs.at[k])
+                go(own(ji, c), own(ji, c), upss.at[p], uprs.at[p], partner)
+
+    def u_from_partner():
+        for own, out, relay, s in kinds:
+            for ji, k, p in u_slots(s):
+                got(own(ji, 1 - c), uprs.at[p])
 
     def tenant_is(b, t, shape):
         return jnp.full(shape, bti[b], jnp.int32) == t
@@ -271,10 +328,10 @@
                 g = jnp.where(tenant_is(b, t, g.shape), gains[t], g)
             gcomp[pl.ds(b * BLOCK, BLOCK), :] = g
 
-    def back_part():
+    def compact(w, a, all_):
         for h in range(2):
-            u = uall[pl.ds(4 * h, 4)].reshape(256, lf)
-            p = dot(cot[...], u, 1, 1)
+            u = all_[pl.ds(4 * h, 4)].reshape(256, a.shape[1])
+            p = dot(a[...], u, 1, 1)
             for b in range(6):
                 rs = slice(b * BLOCK, (b + 1) * BLOCK)
                 acc = jnp.zeros((BLOCK, BLOCK), F32)
@@ -282,15 +339,18 @@
                     acc = jnp.where(
                         tenant_is(b, 4 * h + t, acc.shape), p[rs, 64 * t : 64 * t + 64], acc
                     )
-                at = (slice(rs.start % half, rs.start % half + BLOCK), slice(64 * (b // 3), 64 * (b // 3) + 64))
+                r0, l0 = (b % 3) * BLOCK, 64 * (b // 3)
+                at = (w, slice(r0, r0 + BLOCK), slice(l0, l0 + 64))
                 cp2[at] = acc if h == 0 else cp2[at] + acc
 
     def b_desc(k):
         to = lax.rem(j + k, 8)
-        return rc(cp2.at[pl.ds(to * 24, 24)], brecv.at[k], bss.at[k], brs.at[k], {"tenant": to})
+        return rc(
+            cp2.at[:, pl.ds(to * 24, 24)], brecv.at[k], bss.at[k], brs.at[k], {"tenant": to}
+        )
 
     def b_sum():
-        s = cp2[pl.ds(pl.multiple_of(j * 24, 8), 24), :]
+        s = cp2[:, pl.ds(pl.multiple_of(j * 24, 8), 24), :]
         for k in range(1, 8):
             got(brecv.at[k], brs.at[k])
             s = s + brecv[k]
@@ -302,97 +362,103 @@
     def ag_use():
         for k in range(1, 8):
             got(agx.at[lax.rem(j + 8 - k, 8)], ars.at[k])
-        packed = jnp.concatenate([agx[k] for k in range(8)], axis=0)
-        for b in range(6):
-            r0 = (b % 3) * BLOCK
-            s = packed[r0 : r0 + BLOCK, 64 * (b // 3) : 64 * (b // 3) + 64]
-            v = (s * gcomp[b * BLOCK : (b + 1) * BLOCK, :]).astype(BF).astype(F32)
-            zero = jnp.zeros_like(v)
-            rs = slice(b * BLOCK, (b + 1) * BLOCK)
-            agj[rs, :] = jnp.where(tenant_is(b, j, v.shape), v, zero).astype(BF)
-            for t in range(0, 8, 2):
-                pair = jnp.concatenate(
-                    [jnp.where(tenant_is(b, t + e, v.shape), v, zero) for e in range(2)], axis=1
-                )
-                agexp[rs, 64 * t : 64 * t + 128] = pair.astype(BF)
+        for w, dst in ((0, agexp), (1, aexp)):
+            packed = jnp.concatenate([agx[k, w] for k in range(8)], axis=0)
+            for b in range(6):
+                r0 = (b % 3) * BLOCK
+                s = packed[r0 : r0 + BLOCK, 64 * (b // 3) : 64 * (b // 3) + 64]
+                v = (s * gcomp[b * BLOCK : (b + 1) * BLOCK, :]).astype(BF).astype(F32)
+                zero = jnp.zeros_like(v)
+                rs = slice(b * BLOCK, (b + 1) * BLOCK)
+                if w == 0:
+                    agj[rs, :] = jnp.where(tenant_is(b, j, v.shape), v, zero).astype(BF)
+                for t in range(0, 8, 2):
+                    pair = jnp.concatenate(
+                        [jnp.where(tenant_is(b, t + e, v.shape), v, zero) for e in range(2)], axis=1
+                    )
+                    dst[rs, 64 * t : 64 * t + 128] = pair.astype(BF)
 
     def lhs(q):
         return jnp.concatenate([tokq[i, q] for i in range(8)], axis=1)
 
-    def adapted_part():
-        p = dot(lhs(0), dq[0], 1, 1)
-        for q in range(1, ROUNDS):
-            p = p + dot(lhs(q), dq[q], 1, 1)
-        outs = []
-        for b in range(6):
-            rs = slice(b * BLOCK, (b + 1) * BLOCK)
-            v = p[rs] * gcomp[rs, :]
-            outs.append(jnp.where(tenant_is(b, j, v.shape), v, jnp.zeros_like(v)))
-        for b in range(3):
-            pair = jnp.concatenate([outs[b], outs[b + 3]], axis=1).astype(BF)
-            asend[b * BLOCK : (b + 1) * BLOCK, :] = pair
-            arecv[j, pl.ds(b * BLOCK, BLOCK), :] = pair
-
-    def d_desc(k):
-        return rc(asend, arecv.at[j], dss.at[k], drs.at[k], {"tenant": lax.rem(j + k, 8)})
-
-    def adapted_use():
-        for k in range(1, 8):
-            got(arecv.at[lax.rem(j + 8 - k, 8)], drs.at[k])
-        for t in range(0, 8, 2):
-            a0, a1 = arecv[t], arecv[t + 1]
-            aexp[:half, 64 * t : 64 * t + 128] = jnp.concatenate([a0[:, :64], a1[:, :64]], axis=1)
-            aexp[half:, 64 * t : 64 * t + 128] = jnp.concatenate([a0[:, 64:], a1[:, 64:]], axis=1)
-
     def grad_down_part():
         p = dot(agexp[...], tok[...], 0, 0)
-        gpart[0, :, 0:640] = p[:256]
-        gpart[1, :, 0:640] = p[256:]
-
-    def grad_up_part():
+        gpart[0, :, 0:ld] = p[:256]
+        gpart[1, :, 0:ld] = p[256:]
+
+    def grad_up_part(lo, hi):
         def body(n):
             at = pl.ds(pl.multiple_of(n * 256, 256), 256)
-            to = pl.ds(pl.multiple_of(640 + n * 256, 128), 256)
+            to = pl.ds(pl.multiple_of(ld + n * 256, 128), 256)
             p = dot(aexp[...], cot[:, at], 0, 0)
             gpart[0, :, to] = p[:256]
             gpart[1, :, to] = p[256:]
 
-        each(0, lf // 256, body)
-
-    def rs_make():
-        got(gpr, xrs)
+        each(lo, hi, body)
+
+    fx, fz = f // 2, lax.rem(f, 2)
+    cols = (pl.ds(0, 1152), pl.ds(1152, 1280))
+
+    def gx(p):
+        go(gpart.at[1 - c, :, cols[p]], gpr.at[:, cols[p]], xss.at[p], xrs.at[p], partner)
+
+    def chunk(k, p):
+        at = pl.ds(pl.multiple_of(k * 32, 32), 32)
+        return gpart[c, at, cols[p]] + gpr[at, cols[p]]
+
+    def rs_z(p):
+        got(gpr.at[:, cols[p]], xrs.at[p])
+
+        def body(k):
+            rss[k, :, cols[p]] = chunk(2 * k + 1 - fz, p).astype(BF)
+
+        each(0, 4, body)
+        at = (pl.ds(0, 4), slice(None), cols[p])
+        go(rss.at[at], rsr.at[at], rss_s.at[p, 0], rss_r.at[p, 0], fs("Z"))
+
+    def fx_to(r):
+        return {"fsdp": lax.rem(f + 2 * r, 8)}
+
+    def rs_x(p):
+        got(rsr.at[pl.ds(0, 4), :, cols[p]], rss_r.at[p, 0])
+        for r in range(1, 4):
+            k = lax.rem(fx + r, 4)
+            rss[3 + r, :, cols[p]] = (
+                chunk(2 * k + fz, p) + rsr[k, :, cols[p]].astype(F32)
+            ).astype(BF)
+            at = (3 + r, slice(None), cols[p])
+            go(rss.at[at], rsr.at[at], rss_s.at[p, r], rss_r.at[p, r], fx_to(r))
+
+    def rs_sum(p):
+        s = chunk(f, p) + rsr[fx, :, cols[p]].astype(F32)
+        for r in range(1, 4):
+            got(rsr.at[3 + r, :, cols[p]], rss_r.at[p, r])
+            s = s + rsr[3 + r, :, cols[p]].astype(F32)
+        agg[f, :, cols[p]] = s.astype(BF)
+        ref = agg.at[f, :, cols[p]]
+        for r in range(1, 4):
+            go(ref, ref, ags_s.at[p, r], ags_r.at[p, r], fx_to(r))
+        go(ref, ref, ags_s.at[p, 4], ags_r.at[p, 4], fs("Z"))
+
+    def ag_z(p):
+        for r in range(1, 4):
+            ref = agg.at[lax.rem(f + 8 - 2 * r, 8), :, cols[p]]
+            got(ref, ags_r.at[p, r])
+            go(ref, ref, ags_s.at[p, 4 + r], ags_r.at[p, 4 + r], fs("Z"))
+
+    def grads_out(p):
+        got(agg.at[fn["Z"], :, cols[p]], ags_r.at[p, 4])
+        for r in range(1, 4):
+            got(agg.at[lax.rem(fn["Z"] + 8 - 2 * r, 8), :, cols[p]], ags_r.at[p, 4 + r])
 
         def body(k):
             at = pl.ds(pl.multiple_of(k * 32, 32), 32)
-            rss[k] = (gpart[c, at, :] + gpr[at, :]).astype(BF)
-
-        each(0, 8, body)
-
-    def rs_desc(k):
-        to = lax.rem(f + k, 8)
-        return rc(rss.at[to], rsr.at[k], rss_s.at[k], rss_r.at[k], {"fsdp": to})
-
-    def rs_sum():
-        at = pl.ds(pl.multiple_of(f * 32, 32), 32)
-        for k in range(1, 8):
-            got(rsr.at[k], rss_r.at[k])
-        s = gpart[c, at, :] + gpr[at, :]
-        for k in range(1, 8):
-            s = s + rsr[k].astype(F32)
-        agg[f] = s.astype(BF)
-
-    def gg_desc(k):
-        return rc(agg.at[f], agg.at[f], ags_s.at[k], ags_r.at[k], {"fsdp": lax.rem(f + k, 8)})
-
-    def grads_out():
-        for k in range(1, 8):
-            got(agg.at[lax.rem(f + 8 - k, 8)], ags_r.at[k])
-
-        def body(k):
-            at = pl.ds(pl.multiple_of(k * 32, 32), 32)
-            v = agg[k].astype(F32)
-            gd_out[at, :] = v[:, :640]
-            gu_out[at, :] = v[:, 640:]
+            v = agg[k, :, cols[p]].astype(F32)
+            if p == 0:
+                gd_out[at, :] = v[:, :ld]
+                gu_out[at, 0:512] = v[:, ld:]
+            else:
+                gu_out[at, 512:] = v
 
         each(0, 8, body)
 
@@ -433,11 +499,6 @@
 
         each(0, lf // 256, body)
 
-    def compute(q):
-        w_P(q)
-        compute_g(q)
-        compute_h(q)
-
     def g_sum(q):
         for k in range(3):
             got(grecv.at[q, k], grs.at[q, k])
@@ -468,86 +529,97 @@
         each(0, 6, body)
 
     w_A(0)
+    u_cross()
+    u_own()
+    t_make()
+    t_A()
     w_A(1)
-    each(1, 8, lambda k: u_desc(k).start())
-    t_A()
     make_gain()
+    dq_make()
 
     w_B(0)
     w_C(0)
     w_A(2)
-    t_B()
+    u_fwd()
+    t_Z()
     w_D(0)
+    t_C()
 
     w_B(1)
     w_C(1)
     w_A(3)
-    each(1, 8, u_recv)
-    t_CD("L", "R", 1, 2, 5, 6, 5)
+    u_recv()
+    uloc.wait()
+    dloc.wait()
+    cloc.wait()
+    u_from_partner()
+    compact(0, cot, uall)
+    compact(1, tok, dall)
+    each(1, 8, lambda k: b_desc(k).start())
     w_D(1)
     w_E(0)
-    uloc.wait()
-    cloc.wait()
-    each(1, 8, lambda k: got(u_half(lax.rem(j + 8 - k, 8), 1 - c), uprs.at[k]))
-    back_part()
-    each(1, 8, lambda k: b_desc(k).start())
+    b_sum()
+    each(1, 8, lambda k: ag_desc(k).start())
+    t_B()
 
     w_B(2)
     w_C(2)
     w_A(4)
-    b_sum()
-    each(1, 8, lambda k: ag_desc(k).start())
-    t_CD("LZ", "RZ", 3, 4, 7, 8, 7)
+    ag_use()
+    grad_down_part()
+    grad_up_part(0, 2)
+    gx(0)
+    t_D()
     w_D(2)
     w_E(1)
-    ag_use()
-    kloc.wait()
-    grad_down_part()
-    t_E()
-    dloc.wait()
-    adapted_part()
-    each(1, 8, lambda k: d_desc(k).start())
-    compute(0)
-
+    grad_up_part(2, 7)
+    gx(1)
+    w_P(0)
+    compute_g(0)
+    rs_z(0)
     w_B(3)
     w_C(3)
+    rs_z(1)
+    w_P(1)
+    compute_g(1)
     w_D(3)
     w_E(2)
-    adapted_use()
-    grad_up_part()
-    go(gpart.at[1 - c], gpr, xss, xrs, partner)
-    compute(1)
-
+    rs_x(0)
+    t_E()
+    compute_h(0)
+    g_sum(0)
     w_B(4)
     w_C(4)
-    rs_make()
-    each(1, 8, lambda k: rs_desc(k).start())
+    rs_x(1)
+    w_P(2)
+    compute_g(2)
+    rs_sum(0)
+    compute_h(1)
+    g_sum(1)
+    rs_sum(1)
     w_D(4)
     w_E(3)
-    compute(2)
-    g_sum(0)
-    compute(3)
-    g_sum(1)
-
+    w_P(3)
+    compute_g(3)
+    ag_z(0)
+    compute_h(2)
+    g_sum(2)
+    ag_z(1)
     w_E(4)
-    rs_sum()
-    each(1, 8, lambda k: gg_desc(k).start())
-    g_sum(2)
-    compute(4)
+    w_P(4)
+    compute_g(4)
+    compute_h(3)
     g_sum(3)
+    grads_out(0)
+    compute_h(4)
+    grads_out(1)
     g_sum(4)
-    grads_out()
     gt_final()
 
     for d in sent:
         d.wait_send()
-    each(1, 8, lambda k: u_desc(k).wait_send())
-    each(1, 8, lambda k: up_desc(k).wait_send())
     each(1, 8, lambda k: b_desc(k).wait_send())
     each(1, 8, lambda k: ag_desc(k).wait_send())
-    each(1, 8, lambda k: d_desc(k).wait_send())
-    each(1, 8, lambda k: rs_desc(k).wait_send())
-    each(1, 8, lambda k: gg_desc(k).wait_send())
     for q in range(ROUNDS):
         each(1, 4, lambda k: g_desc(q, lax.rem(y + k, 4)).wait_send())
 
@@ -555,10 +627,8 @@
 def shards(tokens, bti, ranks, w, down, up, cot):
     rows, ld = tokens.shape
     lf = cot.shape[1]
-    d = down.shape[2]
-    tokr = tokens.reshape(rows, 2, ROUNDS, SUB).transpose(2, 0, 1, 3).reshape(ROUNDS, rows, 128)
-    dq = down.reshape(64, 8, 2, ROUNDS, SUB).transpose(3, 0, 1, 2, 4).reshape(ROUNDS, 64, 1024)
-    up = up.reshape(64, up.shape[2])
+    up = up.reshape(up.shape[1:])
+    down = down.reshape(down.shape[1:])
     dma = pltpu.SemaphoreType.DMA
     vm = pltpu.VMEM
     smem = pl.BlockSpec(memory_space=pltpu.SMEM)
@@ -573,7 +643,7 @@
             jax.ShapeDtypeStruct((256, ld), F32),
             jax.ShapeDtypeStruct((256, lf), F32),
         ),
-        in_specs=[smem, smem, hbm, hbm, hbm, hbm, hbm, hbm],
+        in_specs=[smem, smem, hbm, hbm, hbm, hbm, hbm],
         out_specs=(out, out, out, out),
         scratch_shapes=[
             vm((rows, ld), BF),
@@ -581,7 +651,11 @@
             vm((rows, lf), BF),
             vm((ROUNDS, 1024, lf), BF),
             vm((8, ROUNDS, rows, 128), BF),
+            vm((64, 5120), BF),
             vm((8, 64, lf), BF),
+            vm((8, 64, ld), BF),
+            vm((4, 32, lf), BF),
+            vm((4, 32, ld), BF),
             vm((rows, lf), F32),
             vm((ROUNDS, 4, rows, 256), BF),
             vm((ROUNDS, rows, 256), F32),
@@ -589,13 +663,11 @@
             vm((ROUNDS, rows, 128), BF),
             vm((ROUNDS, rows, 128), BF),
             vm((rows, 64), F32),
-            vm((half, 128), F32),
-            vm((8, 24, 128), F32),
-            vm((8, 24, 128), F32),
+            vm((2, half, 128), F32),
+            vm((8, 2, 24, 128), F32),
+            vm((8, 2, 24, 128), F32),
             vm((rows, 64), BF),
             vm((rows, 512), BF),
-            vm((half, 128), BF),
-            vm((8, half, 128), BF),
             vm((rows, 512), BF),
             vm((2, 256, ld + lf), F32),
             vm((256, ld + lf), F32),
@@ -608,12 +680,10 @@
             dma((ROUNDS, 8)),
             dma((9,)),
             dma((9,)),
-            dma((8,)),
-            dma((8,)),
-            dma((8,)),
-            dma((8,)),
-            dma((8,)),
-            dma((8,)),
+            dma((20,)),
+            dma((20,)),
+            dma((17,)),
+            dma((17,)),
             dma((8,)),
             dma((8,)),
             dma((8,)),
@@ -622,17 +692,17 @@
             dma((ROUNDS, 3)),
             dma((ROUNDS,)),
             dma((ROUNDS,)),
-            dma,
-            dma,
-            dma((8,)),
-            dma((8,)),
-            dma((8,)),
-            dma((8,)),
+            dma((2,)),
+            dma((2,)),
+            dma((2, 4)),
+            dma((2, 4)),
+            dma((2, 8)),
+            dma((2, 8)),
         ],
         compiler_params=pltpu.CompilerParams(
             collective_id=0, has_side_effects=True, vmem_limit_bytes=67043328
         ),
-    )(bti, ranks, tokr, tokens, w, dq, up, cot)
+    )(bti, ranks, tokens, w, down, up, cot)
     return hid, gt, gd.reshape(4, 64, ld), gu.reshape(4, 64, lf)
 
 

time: 155 us -> 130 us (0.84)
  Pallas kernels: 142 us -> 124 us
  local copies, waits for them, and re-layouts: 11.7 us -> 5.51 us
    pallas_call x1, Pallas kernels: 142 us -> 124 us  [shards(): pl.pallas_call(kernel, out_shape=(jax.ShapeDtypeStruct((rows, lf), BF), j...]
    reshape x2 -> x0, local copies, waits for them, and re-layouts: 2.69 us -> none  [the longest x1 1.7 us: shards(): down.reshape(64, 8, 2, ROUNDS, SUB).transpose(3, 0, 1, 2, 4)]
    unnamed x14 -> x10, local copies, waits for them, and re-layouts: 7.6 us -> 5.51 us
where the time goes in v2:
time: 130 us
  Pallas kernels  124 us (95%)
  local copies, waits for them, and re-layouts  5.51 us (4%)
    pallas_call x1, Pallas kernels, shards(): pl.pallas_call(kernel, out_shape=(jax.ShapeDtypeStruct((rows, lf), BF), j...  124 us
    unnamed x10, local copies, waits for them, and re-layouts  5.51 us

profile of v2, /device:TPU:1, one launch (start us, length us, event | category | flops | bytes accessed | tf_op | source)
XLA Modules:
  0.0 129.8 jit_solution(822355193410028470)
XLA Ops:
  0.6 123.6 %shard_map.102 = (bf16[384,1792]{1,0:T(8,128)(2,1)}, bf16[384,640]{1,0:T(8,128)(2,1)}, f32[256,640]{1,0:T(8,128)}, f32[256,1792]{1,0:T(8,128)}) custom-call(s32[6]{0:T(128)} %bti.1, s32[8]{0:T(128)} %ranks.1, bf16[384,640]{1,0:T(8,128)(2,1)} %tok_h.1, bf16[320,1792]{1,0:T(8,128)(2,1)} %w_h.1, bf16[64,5120]{1,0:T(8,128)(2,1)} %bitcast.6, ...), custom_call_target="tpu_custom_call" | custom-call | tf_op jit(solution)/shard_map/pallas_call | solution.py:638
  124.2 0.0 copy-start.2
  124.3 0.0 copy-start.1
  124.3 2.6 %copy.15 = bf16[384,1792]{1,0:T(8,128)(2,1)} copy(bf16[384,1792]{1,0:T(8,128)(2,1)} %get-tuple-element.16) | data formatting | bytes 2752512
  126.9 0.0 copy-done.2
  126.9 0.0 copy-start
  126.9 0.8 copy.16
  127.6 0.0 copy-done.1
  127.6 0.8 copy.17
  128.5 0.1 copy-done
  128.5 1.2 copy.18
Async XLA Ops:
  124.2 2.6 %copy-start.2 = (bf16[384,640]{1,0:T(8,128)(2,1)S(1)}, bf16[384,640]{1,0:T(8,128)(2,1)}, u32[]{:S(2)}) copy-start(bf16[384,640]{1,0:T(8,128)(2,1)} %get-tuple-element.17) | copy-start | bytes 1474564
  124.3 3.4 %copy-start.1 = (f32[256,640]{1,0:T(8,128)S(1)}, f32[256,640]{1,0:T(8,128)}, u32[]{:S(2)}) copy-start(f32[256,640]{1,0:T(8,128)} %get-tuple-element.10) | copy-start | bytes 1966084
  126.9 1.7 %copy-start = (f32[256,1792]{1,0:T(8,128)S(1)}, f32[256,1792]{1,0:T(8,128)}, u32[]{:S(2)}) copy-start(f32[256,1792]{1,0:T(8,128)} %get-tuple-element.11) | copy-start | bytes 5505028

commit v3 on v2

--- a/solution.py
+++ b/solution.py
@@ -119,12 +119,11 @@
 
         lax.fori_loop(lo, hi, step, 0)
 
-    sent = []
-
     def go(src, dst, ss, rs, dev):
-        d = rc(src, dst, ss, rs, dev)
-        d.start()
-        sent.append(d)
+        rc(src, dst, ss, rs, dev).start()
+
+    def gone(ref, ss):
+        rc(ref, ref, ss, ss, partner).wait_send()
 
     def got(dst, rs):
         rc(dst, dst, rs, rs, partner).wait_recv()
@@ -135,18 +134,15 @@
     def part(q, fi, ci, h):
         return wall.at[q, pl.ds((2 * fi + ci) * SUB + h * (SUB // 2), SUB // 2)]
 
-    wloc = [
-        pltpu.make_async_copy(w_h.at[pl.ds(q * SUB, SUB)], slot(q, f, c), lsem.at[q])
-        for q in range(ROUNDS)
-    ]
+    wloc = pltpu.make_async_copy(w_h, wall.at[:, pl.ds((2 * f + c) * SUB, SUB)], lsem.at[0])
     ucol = pl.ds(pl.multiple_of(j * lf, 128), lf)
     dcol = pl.ds(pl.multiple_of(j * ld, 128), ld)
-    kloc = pltpu.make_async_copy(tok_h, tok, lsem.at[5])
-    mloc = pltpu.make_async_copy(d_h, dmine, lsem.at[6])
-    uloc = pltpu.make_async_copy(u_h.at[:, ucol], uall.at[j], lsem.at[7])
-    dloc = pltpu.make_async_copy(d_h.at[:, dcol], dall.at[j], lsem.at[8])
-    cloc = pltpu.make_async_copy(cot_h, cot, lsem.at[9])
-    for d in [*wloc, kloc, mloc, uloc, dloc, cloc]:
+    kloc = pltpu.make_async_copy(tok_h, tok, lsem.at[1])
+    mloc = pltpu.make_async_copy(d_h, dmine, lsem.at[2])
+    uloc = pltpu.make_async_copy(u_h.at[:, ucol], uall.at[j], lsem.at[3])
+    dloc = pltpu.make_async_copy(d_h.at[:, dcol], dall.at[j], lsem.at[4])
+    cloc = pltpu.make_async_copy(cot_h, cot, lsem.at[5])
+    for d in [wloc, kloc, mloc, uloc, dloc, cloc]:
         d.start()
 
     barrier = pltpu.get_barrier_semaphore()
@@ -164,56 +160,59 @@
     def fs(i):
         return {"fsdp": fn[i]}
 
-    def w_send(q, name, i, rsem, to, src=None):
+    def w_send(q, name, rsem, to, src=None):
         ref = slot(q, fn[name] if name else f, c) if src is None else src
-        go(ref, ref, wss.at[q, i], rsem, to)
+        go(ref, ref, wss, rsem, to)
 
     def w_got(q, k, ref):
         got(ref, wrs.at[q, k])
 
     def w_A(q):
-        wloc[q].wait()
-        w_send(q, None, 0, wrs.at[q, 1], fs("R"))
-        w_send(q, None, 1, wrs.at[q, 2], fs("L"))
-        w_send(q, None, 2, wrs.at[q, 0], fs("Z"))
-        w_send(q, None, 3, prs.at[q, 0], partner)
+        w_send(q, None, wrs.at[q, 1], fs("R"))
+        w_send(q, None, wrs.at[q, 2], fs("L"))
+        w_send(q, None, wrs.at[q, 0], fs("Z"))
+        w_send(q, None, prs.at[q], partner)
 
     def w_B(q):
         w_got(q, 0, slot(q, fn["Z"], c))
-        w_send(q, "Z", 4, wrs.at[q, 3], fs("R"))
-        w_send(q, "Z", 5, wrs.at[q, 4], fs("L"))
-        w_send(q, "Z", 6, prs.at[q, 1], partner)
-
-    def w_CD(q, left, right, kl, kr, kt, kb, i, p):
+        w_send(q, "Z", wrs.at[q, 3], fs("R"))
+        w_send(q, "Z", wrs.at[q, 4], fs("L"))
+        w_send(q, "Z", prs.at[q], partner)
+
+    def w_CD(q, left, right, kl, kr, ko):
         w_got(q, kl, slot(q, fn[left], c))
-        w_send(q, left, i, wrs.at[q, kt], fs("R"), part(q, fn[left], c, 0))
-        w_send(q, left, i + 1, prs.at[q, p], partner)
+        w_send(q, left, wrs.at[q, ko], fs("R"), part(q, fn[left], c, 0))
+        w_send(q, left, prs.at[q], partner)
         w_got(q, kr, slot(q, fn[right], c))
-        w_send(q, right, i + 2, wrs.at[q, kb], fs("L"), part(q, fn[right], c, 1))
-        w_send(q, right, i + 3, prs.at[q, p + 1], partner)
+        w_send(q, right, wrs.at[q, ko], fs("L"), part(q, fn[right], c, 1))
+        w_send(q, right, prs.at[q], partner)
 
     def w_C(q):
-        w_CD(q, "L", "R", 1, 2, 5, 6, 7, 2)
+        w_CD(q, "L", "R", 1, 2, 5)
 
     def w_D(q):
-        w_CD(q, "LZ", "RZ", 3, 4, 7, 8, 11, 4)
+        w_CD(q, "LZ", "RZ", 3, 4, 6)
 
     def w_E(q):
-        for name, k, i, p in (("O", 5, 15, 6), ("OZ", 7, 16, 7)):
-            w_got(q, k, part(q, fn[name], c, 0))
-            w_got(q, k + 1, part(q, fn[name], c, 1))
-            w_send(q, name, i, prs.at[q, p], partner)
+        for name, k in (("O", 5), ("OZ", 6)):
+            w_got(q, k, slot(q, fn[name], c))
+            w_send(q, name, prs.at[q], partner)
 
     def w_P(q):
-        for p, name in enumerate((None, "Z", "L", "R", "LZ", "RZ", "O", "OZ")):
-            got(slot(q, fn[name] if name else f, 1 - c), prs.at[q, p])
+        got(wall.at[q, pl.ds(0, 8 * SUB)], prs.at[q])
 
     def te(i):
         return {"tenant": tn[i]}
 
-    def t_send(ji, i, k, to, h=None):
-        ref = tokq.at[ji] if h is None else tokq.at[ji, :, pl.ds(h * half, half)]
-        go(ref, ref, tss.at[i], trs.at[k], to)
+    tq = (pl.ds(0, 3), pl.ds(3, 2))
+
+    def t_ref(ji, p, h=None):
+        rows_ = slice(None) if h is None else pl.ds(h * half, half)
+        return tokq.at[ji, tq[p], rows_]
+
+    def t_send(p, ji, k, to, h=None):
+        ref = t_ref(ji, p, h)
+        go(ref, ref, tss, trs.at[p, k], to)
 
     def pieces(v):
         return [
@@ -232,34 +231,33 @@
             for q, v in enumerate(pieces(dmine[:, ld * i : ld * i + ld])):
                 dq[q, :, 128 * i : 128 * i + 128] = v
 
-    def t_A():
-        t_send(j, 0, 1, te("R"))
-        t_send(j, 1, 2, te("L"))
-
-    def t_Z():
-        t_send(j, 2, 0, te("Z"))
-
-    def t_B():
-        got(tokq.at[tn["Z"]], trs.at[0])
-        t_send(tn["Z"], 3, 3, te("R"))
-        t_send(tn["Z"], 4, 4, te("L"))
-
-    def t_CD(left, right, kl, kr, kt, kb, i):
-        got(tokq.at[tn[left]], trs.at[kl])
-        t_send(tn[left], i, kt, te("R"), 0)
-        got(tokq.at[tn[right]], trs.at[kr])
-        t_send(tn[right], i + 1, kb, te("L"), 1)
-
-    def t_C():
-        t_CD("L", "R", 1, 2, 5, 6, 5)
-
-    def t_D():
-        t_CD("LZ", "RZ", 3, 4, 7, 8, 7)
+    def t_A(p):
+        t_send(p, j, 1, te("R"))
+        t_send(p, j, 2, te("L"))
+
+    def t_Z(p):
+        t_send(p, j, 0, te("Z"))
+
+    def t_B(p):
+        got(t_ref(tn["Z"], p), trs.at[p, 0])
+        t_send(p, tn["Z"], 3, te("R"))
+        t_send(p, tn["Z"], 4, te("L"))
+
+    def t_CD(p, left, right, kl, kr):
+        got(t_ref(tn[left], p), trs.at[p, kl])
+        t_send(p, tn[left], 5, te("R"), 0)
+        got(t_ref(tn[right], p), trs.at[p, kr])
+        t_send(p, tn[right], 5, te("L"), 1)
+
+    def t_C(p):
+        t_CD(p, "L", "R", 1, 2)
+
+    def t_D(p):
+        t_CD(p, "LZ", "RZ", 3, 4)
 
     def t_E():
-        for name, k in (("O", 5), ("OZ", 7)):
-            for h in range(2):
-                got(tokq.at[tn[name], :, pl.ds(h * half, half)], trs.at[k + h])
+        for p in range(2):
+            got(tokq.at[pl.ds(0, 2), tq[p]], trs.at[p, 5])
 
     def adapter(src, width, all_, relay, s):
         def own(ji, ci):
@@ -270,7 +268,7 @@
 
         return own, out, relay, s
 
-    kinds = (adapter(d_h, ld, dall, dx, 0), adapter(u_h, lf, uall, ux, 10))
+    kinds = (adapter(d_h, ld, dall, dx, 0), adapter(u_h, lf, uall, ux, 1))
     cross = {"fsdp": fn["Z"], "tenant": tn["Z"]}
 
     def at_y(r):
@@ -278,40 +276,33 @@
 
     def u_cross():
         for own, out, relay, s in kinds:
-            for r in range(4):
+            for r in (1, 2, 3, 0):
                 dst = own(j, c) if r == 0 else relay.at[r]
-                go(out(2 * at_y(r) + 1 - zh), dst, uss.at[s + r], urs.at[s + r], cross)
+                go(out(2 * at_y(r) + 1 - zh), dst, uss.at[s], urs.at[s, r], cross)
 
     def u_own():
         for own, out, relay, s in kinds:
             for r in range(1, 4):
-                to, k = 2 * at_y(r) + zh, s + 3 + r
-                go(out(to), own(j, c), uss.at[k], urs.at[k], {"tenant": to})
+                to = 2 * at_y(r) + zh
+                go(out(to), own(j, c), uss.at[s], urs.at[s, 0], {"tenant": to})
 
     def u_fwd():
         for own, out, relay, s in kinds:
             for r in range(1, 4):
-                got(relay.at[r], urs.at[s + r])
-                to, k = 2 * at_y(r) + zh, s + 6 + r
-                go(relay.at[r], own(tn["Z"], c), uss.at[k], urs.at[k], {"tenant": to})
-
-    def u_slots(s):
-        yield tn["Z"], s, s
-        for r in range(1, 4):
-            yield 2 * at_y(4 - r) + zh, s + 3 + r, s + r
-        for r in range(1, 4):
-            yield 2 * at_y(4 - r) + 1 - zh, s + 6 + r, s + 3 + r
+                got(relay.at[r], urs.at[s, r])
+                to = 2 * at_y(r) + zh
+                go(relay.at[r], own(tn["Z"], c), uss.at[s], urs.at[s, 0], {"tenant": to})
 
     def u_recv():
-        for own, out, relay, s in kinds:
-            for ji, k, p in u_slots(s):
-                got(own(ji, c), urs.at[k])
-                go(own(ji, c), own(ji, c), upss.at[p], uprs.at[p], partner)
+        for (own, out, relay, s), all_ in zip(kinds, (dall, uall)):
+            got(all_.at[pl.ds(0, 7), pl.ds(0, 32)], urs.at[s, 0])
+            for k in range(1, 8):
+                ref = own(lax.rem(j + k, 8), c)
+                go(ref, ref, upss.at[s], uprs.at[s], partner)
 
     def u_from_partner():
-        for own, out, relay, s in kinds:
-            for ji, k, p in u_slots(s):
-                got(own(ji, 1 - c), uprs.at[p])
+        for s, all_ in ((0, dall), (1, uall)):
+            got(all_.at[pl.ds(0, 7), pl.ds(0, 32)], uprs.at[s])
 
     def tenant_is(b, t, shape):
         return jnp.full(shape, bti[b], jnp.int32) == t
@@ -346,22 +337,21 @@
     def b_desc(k):
         to = lax.rem(j + k, 8)
         return rc(
-            cp2.at[:, pl.ds(to * 24, 24)], brecv.at[k], bss.at[k], brs.at[k], {"tenant": to}
+            cp2.at[:, pl.ds(to * 24, 24)], brecv.at[k], bss, brs, {"tenant": to}
         )
 
     def b_sum():
         s = cp2[:, pl.ds(pl.multiple_of(j * 24, 8), 24), :]
+        got(brecv.at[pl.ds(1, 7)], brs)
         for k in range(1, 8):
-            got(brecv.at[k], brs.at[k])
             s = s + brecv[k]
         agx[j] = s
 
     def ag_desc(k):
-        return rc(agx.at[j], agx.at[j], ass_.at[k], ars.at[k], {"tenant": lax.rem(j + k, 8)})
+        return rc(agx.at[j], agx.at[j], ass_, ars, {"tenant": lax.rem(j + k, 8)})
 
     def ag_use():
-        for k in range(1, 8):
-            got(agx.at[lax.rem(j + 8 - k, 8)], ars.at[k])
+        got(agx.at[pl.ds(0, 7)], ars)
         for w, dst in ((0, agexp), (1, aexp)):
             packed = jnp.concatenate([agx[k, w] for k in range(8)], axis=0)
             for b in range(6):
@@ -400,7 +390,7 @@
     cols = (pl.ds(0, 1152), pl.ds(1152, 1280))
 
     def gx(p):
-        go(gpart.at[1 - c, :, cols[p]], gpr.at[:, cols[p]], xss.at[p], xrs.at[p], partner)
+        go(gpart.at[1 - c, :, cols[p]], gpr.at[:, cols[p]], xss, xrs.at[p], partner)
 
     def chunk(k, p):
         at = pl.ds(pl.multiple_of(k * 32, 32), 32)
@@ -414,7 +404,7 @@
 
         each(0, 4, body)
         at = (pl.ds(0, 4), slice(None), cols[p])
-        go(rss.at[at], rsr.at[at], rss_s.at[p, 0], rss_r.at[p, 0], fs("Z"))
+        go(rss.at[at], rsr.at[at], rss_s, rss_r.at[p, 0], fs("Z"))
 
     def fx_to(r):
         return {"fsdp": lax.rem(f + 2 * r, 8)}
@@ -427,29 +417,27 @@
                 chunk(2 * k + fz, p) + rsr[k, :, cols[p]].astype(F32)
             ).astype(BF)
             at = (3 + r, slice(None), cols[p])
-            go(rss.at[at], rsr.at[at], rss_s.at[p, r], rss_r.at[p, r], fx_to(r))
+            go(rss.at[at], rsr.at[at], rss_s, rss_r.at[p, 1], fx_to(r))
 
     def rs_sum(p):
         s = chunk(f, p) + rsr[fx, :, cols[p]].astype(F32)
+        got(rsr.at[pl.ds(4, 3), :, cols[p]], rss_r.at[p, 1])
         for r in range(1, 4):
-            got(rsr.at[3 + r, :, cols[p]], rss_r.at[p, r])
             s = s + rsr[3 + r, :, cols[p]].astype(F32)
         agg[f, :, cols[p]] = s.astype(BF)
         ref = agg.at[f, :, cols[p]]
         for r in range(1, 4):
-            go(ref, ref, ags_s.at[p, r], ags_r.at[p, r], fx_to(r))
-        go(ref, ref, ags_s.at[p, 4], ags_r.at[p, 4], fs("Z"))
+            go(ref, ref, ags_s, ags_r.at[p, 0], fx_to(r))
+        go(ref, ref, ags_s, ags_r.at[p, 1], fs("Z"))
 
     def ag_z(p):
+        got(agg.at[pl.ds(0, 3), :, cols[p]], ags_r.at[p, 0])
         for r in range(1, 4):
             ref = agg.at[lax.rem(f + 8 - 2 * r, 8), :, cols[p]]
-            got(ref, ags_r.at[p, r])
-            go(ref, ref, ags_s.at[p, 4 + r], ags_r.at[p, 4 + r], fs("Z"))
+            go(ref, ref, ags_s, ags_r.at[p, 1], fs("Z"))
 
     def grads_out(p):
-        got(agg.at[fn["Z"], :, cols[p]], ags_r.at[p, 4])
-        for r in range(1, 4):
-            got(agg.at[lax.rem(fn["Z"] + 8 - 2 * r, 8), :, cols[p]], ags_r.at[p, 4 + r])
+        got(agg.at[pl.ds(0, 4), :, cols[p]], ags_r.at[p, 1])
 
         def body(k):
             at = pl.ds(pl.multiple_of(k * 32, 32), 32)
@@ -465,7 +453,7 @@
     def g_desc(q, i):
         rel = lax.rem(y - i + 4, 4) - 1
         return rc(
-            gsend.at[q, i], grecv.at[q, rel], gss.at[q, i], grs.at[q, rel], {"tenant": 2 * i + zh}
+            gsend.at[q, i], grecv.at[q, rel], gss, grs.at[q], {"tenant": 2 * i + zh}
         )
 
     def compute_g(q):
@@ -500,8 +488,7 @@
         each(0, lf // 256, body)
 
     def g_sum(q):
-        for k in range(3):
-            got(grecv.at[q, k], grs.at[q, k])
+        got(grecv.at[q], grs.at[q])
         mine = pl.ds(pl.multiple_of(zh * 128, 128), 128)
         other = pl.ds(pl.multiple_of(128 - zh * 128, 128), 128)
 
@@ -512,13 +499,12 @@
             return s
 
         gzs[q] = total(other).astype(BF)
-        go(gzs.at[q], gzr.at[q], zss.at[q], zrs.at[q], te("Z"))
+        go(gzs.at[q], gzr.at[q], zss, zrs, te("Z"))
         gown[q, :, mine] = total(mine)
 
     def gt_final():
         mine = pl.ds(pl.multiple_of(zh * 128, 128), 128)
-        for q in range(ROUNDS):
-            got(gzr.at[q], zrs.at[q])
+        got(gzr, zrs)
 
         def body(b):
             at = pl.ds(pl.multiple_of(b * BLOCK, BLOCK), BLOCK)
@@ -528,27 +514,29 @@
 
         each(0, 6, body)
 
+    wloc.wait()
     w_A(0)
     u_cross()
     u_own()
+    w_A(1)
     t_make()
-    t_A()
-    w_A(1)
+    t_A(0)
     make_gain()
     dq_make()
-
     w_B(0)
     w_C(0)
     w_A(2)
     u_fwd()
-    t_Z()
+    t_A(1)
+    t_Z(0)
+    t_Z(1)
+    t_C(0)
     w_D(0)
-    t_C()
-
     w_B(1)
     w_C(1)
     w_A(3)
     u_recv()
+    t_B(0)
     uloc.wait()
     dloc.wait()
     cloc.wait()
@@ -556,78 +544,86 @@
     compact(0, cot, uall)
     compact(1, tok, dall)
     each(1, 8, lambda k: b_desc(k).start())
+    t_C(1)
+    w_E(0)
+    w_B(2)
+    w_C(2)
     w_D(1)
-    w_E(0)
     b_sum()
     each(1, 8, lambda k: ag_desc(k).start())
-    t_B()
-
-    w_B(2)
-    w_C(2)
+    t_B(1)
     w_A(4)
+    t_D(0)
     ag_use()
+    w_P(0)
+    compute_g(0)
+    t_D(1)
+    w_E(1)
+    w_P(1)
+    compute_g(1)
+    w_D(2)
+    w_B(3)
+    w_C(3)
     grad_down_part()
     grad_up_part(0, 2)
     gx(0)
-    t_D()
-    w_D(2)
-    w_E(1)
     grad_up_part(2, 7)
     gx(1)
-    w_P(0)
-    compute_g(0)
+    w_E(2)
+    w_P(2)
+    compute_g(2)
     rs_z(0)
-    w_B(3)
-    w_C(3)
     rs_z(1)
-    w_P(1)
-    compute_g(1)
+    g_sum(0)
     w_D(3)
-    w_E(2)
-    rs_x(0)
+    w_B(4)
+    w_C(4)
     t_E()
     compute_h(0)
-    g_sum(0)
-    w_B(4)
-    w_C(4)
-    rs_x(1)
-    w_P(2)
-    compute_g(2)
-    rs_sum(0)
-    compute_h(1)
-    g_sum(1)
-    rs_sum(1)
-    w_D(4)
     w_E(3)
     w_P(3)
     compute_g(3)
-    ag_z(0)
-    compute_h(2)
-    g_sum(2)
-    ag_z(1)
+    w_D(4)
+    rs_x(0)
+    rs_x(1)
+    g_sum(1)
+    compute_h(1)
     w_E(4)
     w_P(4)
     compute_g(4)
+    rs_sum(0)
+    rs_sum(1)
+    g_sum(2)
+    compute_h(2)
+    ag_z(0)
+    ag_z(1)
     compute_h(3)
     g_sum(3)
+    compute_h(4)
     grads_out(0)
-    compute_h(4)
     grads_out(1)
     g_sum(4)
     gt_final()
 
-    for d in sent:
-        d.wait_send()
-    each(1, 8, lambda k: b_desc(k).wait_send())
-    each(1, 8, lambda k: ag_desc(k).wait_send())
-    for q in range(ROUNDS):
-        each(1, 4, lambda k: g_desc(q, lax.rem(y + k, 4)).wait_send())
+    gone(wall.at[:, pl.ds(0, 15 * SUB)], wss)
+    gone(tokq.at[pl.ds(0, 7)], tss)
+    for s, all_ in ((0, dall), (1, uall)):
+        gone(all_.at[pl.ds(0, 5)], uss.at[s])
+        gone(all_.at[pl.ds(0, 7), pl.ds(0, 32)], upss.at[s])
+    gone(brecv.at[pl.ds(0, 7)], bss)
+    gone(agx.at[pl.ds(0, 7)], ass_)
+    gone(gsend.at[:, pl.ds(0, 3)], gss)
+    gone(gzs, zss)
+    gone(gpr, xss)
+    gone(rss.at[pl.ds(0, 7)], rss_s)
+    gone(agg.at[pl.ds(0, 7)], ags_s)
 
 
 def shards(tokens, bti, ranks, w, down, up, cot):
     rows, ld = tokens.shape
     lf = cot.shape[1]
     up = up.reshape(up.shape[1:])
+    w = w.reshape(ROUNDS, SUB, lf)
     down = down.reshape(down.shape[1:])
     dma = pltpu.SemaphoreType.DMA
     vm = pltpu.VMEM
@@ -638,10 +634,10 @@
     hid, gt, gd, gu = pl.pallas_call(
         kernel,
         out_shape=(
-            jax.ShapeDtypeStruct((rows, lf), BF),
-            jax.ShapeDtypeStruct((rows, ld), BF),
-            jax.ShapeDtypeStruct((256, ld), F32),
-            jax.ShapeDtypeStruct((256, lf), F32),
+            pltpu.VMEM((rows, lf), BF),
+            pltpu.VMEM((rows, ld), BF),
+            pltpu.VMEM((256, ld), F32),
+            pltpu.VMEM((256, lf), F32),
         ),
         in_specs=[smem, smem, hbm, hbm, hbm, hbm, hbm],
         out_specs=(out, out, out, out),
@@ -674,33 +670,33 @@
             vm((8, 32, ld + lf), BF),
             vm((8, 32, ld + lf), BF),
             vm((8, 32, ld + lf), BF),
-            dma((10,)),
-            dma((ROUNDS, 17)),
-            dma((ROUNDS, 9)),
-            dma((ROUNDS, 8)),
-            dma((9,)),
-            dma((9,)),
-            dma((20,)),
-            dma((20,)),
-            dma((17,)),
-            dma((17,)),
-            dma((8,)),
-            dma((8,)),
-            dma((8,)),
-            dma((8,)),
-            dma((ROUNDS, 4)),
-            dma((ROUNDS, 3)),
+            dma((6,)),
+            dma,
+            dma((ROUNDS, 7)),
             dma((ROUNDS,)),
-            dma((ROUNDS,)),
+            dma,
+            dma((2, 6)),
+            dma((2,)),
+            dma((2, 4)),
             dma((2,)),
             dma((2,)),
-            dma((2, 4)),
-            dma((2, 4)),
-            dma((2, 8)),
-            dma((2, 8)),
+            dma,
+            dma,
+            dma,
+            dma,
+            dma,
+            dma((ROUNDS,)),
+            dma,
+            dma,
+            dma,
+            dma((2,)),
+            dma,
+            dma((2, 2)),
+            dma,
+            dma((2, 2)),
         ],
         compiler_params=pltpu.CompilerParams(
-            collective_id=0, has_side_effects=True, vmem_limit_bytes=67043328
+            collective_id=0, has_side_effects=True, vmem_limit_bytes=58 << 20
         ),
     )(bti, ranks, tokens, w, down, up, cot)
     return hid, gt, gd.reshape(4, 64, ld), gu.reshape(4, 64, lf)

time: 130 us -> 123 us (0.946)
  Pallas kernels: 124 us -> 118 us
  local copies, waits for them, and re-layouts: 5.51 us -> 3.92 us
    pallas_call x1, Pallas kernels: 124 us -> 118 us  [shards(): pl.pallas_call(kernel, out_shape=(pltpu.VMEM((rows, lf), BF), pltpu.VMEM(...]
    unnamed x10 -> x4, local copies, waits for them, and re-layouts: 5.51 us -> 3.92 us
where the time goes in v3:
time: 123 us; the launch traced here: 122 us
  Pallas kernels  118 us (96%)
  local copies, waits for them, and re-layouts  3.92 us (3%)
    pallas_call x1, Pallas kernels, shards(): pl.pallas_call(kernel, out_shape=(pltpu.VMEM((rows, lf), BF), pltpu.VMEM(...  118 us
    unnamed x4, local copies, waits for them, and re-layouts  3.92 us

profile of v3, /device:TPU:1, one launch (start us, length us, event | category | flops | bytes accessed | tf_op | source)
XLA Modules:
  0.0 122.5 jit_solution(4870833112284312987)
XLA Ops:
  0.6 117.9 %shard_map.102 = (bf16[384,1792]{1,0:T(8,128)(2,1)S(1)}, bf16[384,640]{1,0:T(8,128)(2,1)S(1)}, f32[256,640]{1,0:T(8,128)S(1)}, f32[256,1792]{1,0:T(8,128)S(1)}) custom-call(s32[6]{0:T(128)} %bti.1, s32[8]{0:T(128)} %ranks.1, bf16[384,640]{1,0:T(8,128)(2,1)} %tok_h.1, bf16[5,64,1792]{2,1,0:T(8,128)(2,1)} %bitcast.8, bf16[64,5120]{1,0:T(8,128)(2,1)} %bitcast.9, ...), custom_call_target="tpu_custom_call" | custom-call | tf_op jit(solution)/shard_map/pallas_call | solution.py:634
  118.6 1.1 copy.15
  119.6 0.8 copy.16
  120.4 0.8 copy.17
  121.2 1.2 %copy.18 = f32[4,64,1792]{2,1,0:T(8,128)} copy(f32[4,64,1792]{2,1,0:T(8,128)S(1)} %bitcast.5) | data formatting | bytes 3670016

commit v4 on v3

--- a/solution.py
+++ b/solution.py
@@ -41,7 +41,10 @@
     ux,
     dx,
     hacc,
-    gsend,
+    gopp,
+    gn,
+    gf,
+    gor,
     gown,
     grecv,
     gzs,
@@ -72,7 +75,9 @@
     brs,
     ass_,
     ars,
-    gss,
+    gos,
+    gors,
+    gns,
     grs,
     zss,
     zrs,
@@ -155,7 +160,6 @@
     pl.semaphore_signal(
         barrier, 1, device_id={"fsdp": fn["Z"], "tenant": tn["Z"]}, device_id_type=MESH
     )
-    pl.semaphore_wait(barrier, 16)
 
     def fs(i):
         return {"fsdp": fn[i]}
@@ -198,6 +202,27 @@
             w_got(q, k, slot(q, fn[name], c))
             w_send(q, name, prs.at[q], partner)
 
+    def x_C(q):
+        for name, k, h, kz, to in (("L", 1, 0, 3, "R"), ("R", 2, 1, 4, "L")):
+            w_got(q, k, slot(q, fn[name], c))
+            w_send(q, name, wrs.at[q, 5], fs(to), part(q, fn[name], c, h))
+            w_send(q, name, wrs.at[q, kz], fs("Z"))
+            w_send(q, name, prs.at[q], partner)
+
+    def x_D(q):
+        for name, k in (("Z", 0), ("LZ", 3), ("RZ", 4)):
+            w_got(q, k, slot(q, fn[name], c))
+            w_send(q, name, prs.at[q], partner)
+
+    def x_O(q):
+        w_got(q, 5, slot(q, fn["O"], c))
+        w_send(q, "O", wrs.at[q, 6], fs("Z"))
+        w_send(q, "O", prs.at[q], partner)
+
+    def x_E(q):
+        w_got(q, 6, slot(q, fn["OZ"], c))
+        w_send(q, "OZ", prs.at[q], partner)
+
     def w_P(q):
         got(wall.at[q, pl.ds(0, 8 * SUB)], prs.at[q])
 
@@ -291,14 +316,14 @@
             for r in range(1, 4):
                 got(relay.at[r], urs.at[s, r])
                 to = 2 * at_y(r) + zh
-                go(relay.at[r], own(tn["Z"], c), uss.at[s], urs.at[s, 0], {"tenant": to})
-
-    def u_recv():
+                go(relay.at[r], own(tn["Z"], c), uss.at[s], urs.at[s, 4], {"tenant": to})
+
+    def u_recv(e):
         for (own, out, relay, s), all_ in zip(kinds, (dall, uall)):
-            got(all_.at[pl.ds(0, 7), pl.ds(0, 32)], urs.at[s, 0])
-            for k in range(1, 8):
-                ref = own(lax.rem(j + k, 8), c)
-                go(ref, ref, upss.at[s], uprs.at[s], partner)
+            got(all_.at[pl.ds(0, 4 - e), pl.ds(0, 32)], urs.at[s, 4 * e])
+            for r in range(e, 4):
+                ji = 2 * at_y(4 - r) + (1 - zh if e == 1 or r == 0 else zh)
+                go(own(ji, c), own(ji, c), upss.at[s], uprs.at[s], partner)
 
     def u_from_partner():
         for s, all_ in ((0, dall), (1, uall)):
@@ -387,7 +412,7 @@
         each(lo, hi, body)
 
     fx, fz = f // 2, lax.rem(f, 2)
-    cols = (pl.ds(0, 1152), pl.ds(1152, 1280))
+    cols = (pl.ds(0, 896), pl.ds(896, 1536))
 
     def gx(p):
         go(gpart.at[1 - c, :, cols[p]], gpr.at[:, cols[p]], xss, xrs.at[p], partner)
@@ -419,6 +444,10 @@
             at = (3 + r, slice(None), cols[p])
             go(rss.at[at], rsr.at[at], rss_s, rss_r.at[p, 1], fx_to(r))
 
+    def to_x(ref, sem):
+        for r in range(1, 4):
+            go(ref, ref, ags_s, sem, fx_to(r))
+
     def rs_sum(p):
         s = chunk(f, p) + rsr[fx, :, cols[p]].astype(F32)
         got(rsr.at[pl.ds(4, 3), :, cols[p]], rss_r.at[p, 1])
@@ -426,52 +455,77 @@
             s = s + rsr[3 + r, :, cols[p]].astype(F32)
         agg[f, :, cols[p]] = s.astype(BF)
         ref = agg.at[f, :, cols[p]]
+        go(ref, ref, ags_s, ags_r.at[p, 1], fs("Z"))
+        to_x(ref, ags_r.at[p, 0])
+
+    def ag_z():
+        got(agg.at[pl.ds(0, 3), :, cols[0]], ags_r.at[0, 0])
         for r in range(1, 4):
-            go(ref, ref, ags_s, ags_r.at[p, 0], fx_to(r))
-        go(ref, ref, ags_s, ags_r.at[p, 1], fs("Z"))
-
-    def ag_z(p):
-        got(agg.at[pl.ds(0, 3), :, cols[p]], ags_r.at[p, 0])
-        for r in range(1, 4):
-            ref = agg.at[lax.rem(f + 8 - 2 * r, 8), :, cols[p]]
-            go(ref, ref, ags_s, ags_r.at[p, 1], fs("Z"))
+            ref = agg.at[lax.rem(f + 8 - 2 * r, 8), :, cols[0]]
+            go(ref, ref, ags_s, ags_r.at[0, 1], fs("Z"))
+
+    def ag_x():
+        ref = agg.at[fn["Z"], :, cols[1]]
+        got(ref, ags_r.at[1, 1])
+        to_x(ref, ags_r.at[1, 0])
 
     def grads_out(p):
-        got(agg.at[pl.ds(0, 4), :, cols[p]], ags_r.at[p, 1])
+        if p == 0:
+            got(agg.at[pl.ds(0, 4), :, cols[p]], ags_r.at[p, 1])
+        else:
+            got(agg.at[pl.ds(0, 6), :, cols[p]], ags_r.at[p, 0])
 
         def body(k):
             at = pl.ds(pl.multiple_of(k * 32, 32), 32)
             v = agg[k, :, cols[p]].astype(F32)
             if p == 0:
                 gd_out[at, :] = v[:, :ld]
-                gu_out[at, 0:512] = v[:, ld:]
+                gu_out[at, 0:256] = v[:, ld:]
             else:
-                gu_out[at, 512:] = v
+                gu_out[at, 256:] = v
 
         each(0, 8, body)
 
-    def g_desc(q, i):
-        rel = lax.rem(y - i + 4, 4) - 1
-        return rc(
-            gsend.at[q, i], grecv.at[q, rel], gss, grs.at[q], {"tenant": 2 * i + zh}
-        )
+    top, bottom = pl.ds(0, half), pl.ds(half, half)
+
+    def g_near(q, e, at):
+        go(gn.at[q, e, at], grecv.at[q, e, at], gns, grs.at[q], te("RL"[e]))
 
     def compute_g(q):
         def body(k):
-            i = lax.rem(y + k, 4)
+            i = lax.rem(y + 2 + 3 * k, 4)
             at = pl.ds(pl.multiple_of(i * 256, 256), 256)
             p = dot(cot[...], wall[q, at, :], 1, 1) + dot(agj[...], dq[q, :, at], 1, 0)
 
-            @pl.when(k < 4)
+            @pl.when(k == 0)
             def _():
-                gsend[q, i] = p.astype(BF)
-                g_desc(q, i).start()
-
-            @pl.when(k == 4)
+                gopp[q] = p.astype(BF)
+                go(gopp.at[q, top], gor.at[q, 0], gos, gors.at[q], te("R"))
+                go(gopp.at[q, bottom], gor.at[q, 1], gos, gors.at[q], te("L"))
+
+            @pl.when(k == 1)
+            def _():
+                gf[q, 0] = p[:half]
+                gn[q, 0, half:] = p[half:].astype(BF)
+                g_near(q, 0, bottom)
+
+            @pl.when(k == 2)
             def _():
                 gown[q] = p
 
-        each(1, 5, body)
+            @pl.when(k == 3)
+            def _():
+                gf[q, 1] = p[half:]
+                gn[q, 1, :half] = p[:half].astype(BF)
+                g_near(q, 1, top)
+
+        each(0, 4, body)
+
+    def g_acc(q):
+        got(gor.at[q], gors.at[q])
+        for e, at in enumerate((top, bottom)):
+            gn[q, e, at] = (gf[q, e] + gor[q, e].astype(F32)).astype(BF)
+            g_near(q, e, at)
 
     def compute_h(q):
         def body(n):
@@ -494,7 +548,7 @@
 
         def total(at):
             s = gown[q, :, at]
-            for k in range(3):
+            for k in range(2):
                 s = s + grecv[q, k, :, at].astype(F32)
             return s
 
@@ -514,15 +568,16 @@
 
         each(0, 6, body)
 
+    t_make()
+    dq_make()
+    make_gain()
     wloc.wait()
+    pl.semaphore_wait(barrier, 16)
     w_A(0)
     u_cross()
     u_own()
     w_A(1)
-    t_make()
     t_A(0)
-    make_gain()
-    dq_make()
     w_B(0)
     w_C(0)
     w_A(2)
@@ -531,12 +586,12 @@
     t_Z(0)
     t_Z(1)
     t_C(0)
+    u_recv(0)
     w_D(0)
     w_B(1)
     w_C(1)
     w_A(3)
-    u_recv()
-    t_B(0)
+    u_recv(1)
     uloc.wait()
     dloc.wait()
     cloc.wait()
@@ -546,63 +601,69 @@
     each(1, 8, lambda k: b_desc(k).start())
     t_C(1)
     w_E(0)
-    w_B(2)
-    w_C(2)
-    w_D(1)
     b_sum()
     each(1, 8, lambda k: ag_desc(k).start())
+    t_B(0)
     t_B(1)
     w_A(4)
-    t_D(0)
+    w_D(1)
+    x_C(2)
     ag_use()
     w_P(0)
     compute_g(0)
-    t_D(1)
-    w_E(1)
-    w_P(1)
-    compute_g(1)
-    w_D(2)
     w_B(3)
     w_C(3)
     grad_down_part()
-    grad_up_part(0, 2)
+    grad_up_part(0, 1)
     gx(0)
-    grad_up_part(2, 7)
+    grad_up_part(1, 7)
     gx(1)
-    w_E(2)
+    w_E(1)
+    t_D(0)
+    w_B(4)
+    x_O(2)
+    rs_z(0)
+    t_D(1)
+    w_P(1)
+    compute_g(1)
+    g_acc(0)
+    x_D(2)
+    w_D(3)
+    w_C(4)
+    rs_z(1)
+    t_E()
+    compute_h(0)
+    x_E(2)
+    w_D(4)
     w_P(2)
     compute_g(2)
-    rs_z(0)
-    rs_z(1)
-    g_sum(0)
-    w_D(3)
-    w_B(4)
-    w_C(4)
-    t_E()
-    compute_h(0)
+    g_acc(1)
+    compute_h(1)
     w_E(3)
     w_P(3)
     compute_g(3)
-    w_D(4)
     rs_x(0)
     rs_x(1)
-    g_sum(1)
-    compute_h(1)
+    g_sum(0)
+    g_acc(2)
     w_E(4)
     w_P(4)
     compute_g(4)
+    g_sum(1)
+    compute_h(2)
+    g_acc(3)
     rs_sum(0)
     rs_sum(1)
+    g_acc(4)
     g_sum(2)
-    compute_h(2)
-    ag_z(0)
-    ag_z(1)
     compute_h(3)
+    ag_x()
     g_sum(3)
+    g_sum(4)
+    ag_z()
     compute_h(4)
+    grads_out(1)
     grads_out(0)
-    grads_out(1)
-    g_sum(4)
     gt_final()
 
     gone(wall.at[:, pl.ds(0, 15 * SUB)], wss)
@@ -612,7 +673,8 @@
         gone(all_.at[pl.ds(0, 7), pl.ds(0, 32)], upss.at[s])
     gone(brecv.at[pl.ds(0, 7)], bss)
     gone(agx.at[pl.ds(0, 7)], ass_)
-    gone(gsend.at[:, pl.ds(0, 3)], gss)
+    gone(gopp, gos)
+    gone(gn, gns)
     gone(gzs, zss)
     gone(gpr, xss)
     gone(rss.at[pl.ds(0, 7)], rss_s)
@@ -653,9 +715,12 @@
             vm((4, 32, lf), BF),
             vm((4, 32, ld), BF),
             vm((rows, lf), F32),
-            vm((ROUNDS, 4, rows, 256), BF),
+            vm((ROUNDS, rows, 256), BF),
+            vm((ROUNDS, 2, rows, 256), BF),
+            vm((ROUNDS, 2, half, 256), F32),
+            vm((ROUNDS, 2, half, 256), BF),
             vm((ROUNDS, rows, 256), F32),
-            vm((ROUNDS, 3, rows, 256), BF),
+            vm((ROUNDS, 2, rows, 256), BF),
             vm((ROUNDS, rows, 128), BF),
             vm((ROUNDS, rows, 128), BF),
             vm((rows, 64), F32),
@@ -677,13 +742,15 @@
             dma,
             dma((2, 6)),
             dma((2,)),
-            dma((2, 4)),
+            dma((2, 5)),
             dma((2,)),
             dma((2,)),
             dma,
             dma,
             dma,
             dma,
+            dma,
+            dma((ROUNDS,)),
             dma,
             dma((ROUNDS,)),
             dma,

time: 123 us -> 110 us (0.89)
  Pallas kernels: 118 us -> 105 us
    pallas_call x1, Pallas kernels: 118 us -> 105 us  [shards(): pl.pallas_call(kernel, out_shape=(pltpu.VMEM((rows, lf), BF), pltpu.VMEM(...]
where the time goes in v4:
time: 110 us
  Pallas kernels  105 us (95%)
  local copies, waits for them, and re-layouts  3.92 us (4%)
    pallas_call x1, Pallas kernels, shards(): pl.pallas_call(kernel, out_shape=(pltpu.VMEM((rows, lf), BF), pltpu.VMEM(...  105 us
    unnamed x4, local copies, waits for them, and re-layouts  3.92 us

profile of v4, /device:TPU:1, one launch (start us, length us, event | category | flops | bytes accessed | tf_op | source)
XLA Modules:
  0.0 110.0 jit_solution(14464806513900623364)
XLA Ops:
  0.6 105.5 %shard_map.102 = (bf16[384,1792]{1,0:T(8,128)(2,1)S(1)}, bf16[384,640]{1,0:T(8,128)(2,1)S(1)}, f32[256,640]{1,0:T(8,128)S(1)}, f32[256,1792]{1,0:T(8,128)S(1)}) custom-call(s32[6]{0:T(128)} %bti.1, s32[8]{0:T(128)} %ranks.1, bf16[384,640]{1,0:T(8,128)(2,1)} %tok_h.1, bf16[5,64,1792]{2,1,0:T(8,128)(2,1)} %bitcast.8, bf16[64,5120]{1,0:T(8,128)(2,1)} %bitcast.9, ...), custom_call_target="tpu_custom_call" | custom-call | tf_op jit(solution)/shard_map/pallas_call | solution.py:696
  106.1 1.1 copy.15
  107.2 0.8 copy.16
  108.0 0.8 copy.17
  108.8 1.2 %copy.18 = f32[4,64,1792]{2,1,0:T(8,128)} copy(f32[4,64,1792]{2,1,0:T(8,128)S(1)} %bitcast.5) | data formatting | bytes 3670016

commit v5 on v4

--- a/solution.py
+++ b/solution.py
@@ -133,6 +133,17 @@
     def got(dst, rs):
         rc(dst, dst, rs, rs, partner).wait_recv()
 
+    barrier = pltpu.get_barrier_semaphore()
+    for k in range(1, 8):
+        pl.semaphore_signal(barrier, 1, device_id={"fsdp": lax.rem(f + k, 8)}, device_id_type=MESH)
+        pl.semaphore_signal(
+            barrier, 1, device_id={"tenant": lax.rem(j + k, 8)}, device_id_type=MESH
+        )
+    pl.semaphore_signal(barrier, 1, device_id=partner, device_id_type=MESH)
+    pl.semaphore_signal(
+        barrier, 1, device_id={"fsdp": fn["Z"], "tenant": tn["Z"]}, device_id_type=MESH
+    )
+
     def slot(q, fi, ci):
         return wall.at[q, pl.ds((2 * fi + ci) * SUB, SUB)]
 
@@ -150,17 +161,6 @@
     for d in [wloc, kloc, mloc, uloc, dloc, cloc]:
         d.start()
 
-    barrier = pltpu.get_barrier_semaphore()
-    for k in range(1, 8):
-        pl.semaphore_signal(barrier, 1, device_id={"fsdp": lax.rem(f + k, 8)}, device_id_type=MESH)
-        pl.semaphore_signal(
-            barrier, 1, device_id={"tenant": lax.rem(j + k, 8)}, device_id_type=MESH
-        )
-    pl.semaphore_signal(barrier, 1, device_id=partner, device_id_type=MESH)
-    pl.semaphore_signal(
-        barrier, 1, device_id={"fsdp": fn["Z"], "tenant": tn["Z"]}, device_id_type=MESH
-    )
-
     def fs(i):
         return {"fsdp": fn[i]}
 
@@ -333,13 +333,14 @@
         return jnp.full(shape, bti[b], jnp.int32) == t
 
     def make_gain():
-        lane = lax.broadcasted_iota(jnp.int32, (BLOCK, BLOCK), 1)
+        shape = (BLOCK, 128)
+        slot_ = lax.rem(lax.broadcasted_iota(jnp.int32, shape, 1), 64)
         gains = []
         for t in range(8):
-            r = jnp.full((BLOCK, BLOCK), ranks[t], jnp.int32)
-            gains.append(jnp.where(lane < r, ALPHA / r.astype(F32), 0.0))
+            r = jnp.full(shape, ranks[t], jnp.int32)
+            gains.append(jnp.where(slot_ < r, ALPHA / r.astype(F32), 0.0))
         for b in range(6):
-            g = jnp.zeros((BLOCK, BLOCK), F32)
+            g = jnp.zeros(shape, F32)
             for t in range(8):
                 g = jnp.where(tenant_is(b, t, g.shape), gains[t], g)
             gcomp[pl.ds(b * BLOCK, BLOCK), :] = g
@@ -355,36 +356,32 @@
                     acc = jnp.where(
                         tenant_is(b, 4 * h + t, acc.shape), p[rs, 64 * t : 64 * t + 64], acc
                     )
-                r0, l0 = (b % 3) * BLOCK, 64 * (b // 3)
-                at = (w, slice(r0, r0 + BLOCK), slice(l0, l0 + 64))
+                at = (rs, slice(64 * w, 64 * w + 64))
                 cp2[at] = acc if h == 0 else cp2[at] + acc
 
     def b_desc(k):
         to = lax.rem(j + k, 8)
-        return rc(
-            cp2.at[:, pl.ds(to * 24, 24)], brecv.at[k], bss, brs, {"tenant": to}
-        )
+        return rc(cp2.at[pl.ds(to * 48, 48)], brecv.at[k], bss, brs, {"tenant": to})
 
     def b_sum():
-        s = cp2[:, pl.ds(pl.multiple_of(j * 24, 8), 24), :]
+        at = pl.ds(pl.multiple_of(j * 48, 16), 48)
+        s = cp2[at, :]
         got(brecv.at[pl.ds(1, 7)], brs)
         for k in range(1, 8):
             s = s + brecv[k]
-        agx[j] = s
+        agx[j] = (s * gcomp[at, :]).astype(BF)
 
     def ag_desc(k):
         return rc(agx.at[j], agx.at[j], ass_, ars, {"tenant": lax.rem(j + k, 8)})
 
     def ag_use():
         got(agx.at[pl.ds(0, 7)], ars)
+        both = jnp.concatenate([agx[k] for k in range(8)], axis=0).astype(F32)
         for w, dst in ((0, agexp), (1, aexp)):
-            packed = jnp.concatenate([agx[k, w] for k in range(8)], axis=0)
             for b in range(6):
-                r0 = (b % 3) * BLOCK
-                s = packed[r0 : r0 + BLOCK, 64 * (b // 3) : 64 * (b // 3) + 64]
-                v = (s * gcomp[b * BLOCK : (b + 1) * BLOCK, :]).astype(BF).astype(F32)
+                rs = slice(b * BLOCK, (b + 1) * BLOCK)
+                v = both[rs, 64 * w : 64 * w + 64]
                 zero = jnp.zeros_like(v)
-                rs = slice(b * BLOCK, (b + 1) * BLOCK)
                 if w == 0:
                     agj[rs, :] = jnp.where(tenant_is(b, j, v.shape), v, zero).astype(BF)
                 for t in range(0, 8, 2):
@@ -631,36 +628,36 @@
     w_D(3)
     w_C(4)
     rs_z(1)
-    t_E()
-    compute_h(0)
     x_E(2)
-    w_D(4)
     w_P(2)
     compute_g(2)
     g_acc(1)
-    compute_h(1)
+    w_D(4)
+    t_E()
+    compute_h(0)
     w_E(3)
+    rs_x(0)
     w_P(3)
     compute_g(3)
-    rs_x(0)
+    g_acc(2)
     rs_x(1)
     g_sum(0)
-    g_acc(2)
     w_E(4)
+    compute_h(1)
     w_P(4)
     compute_g(4)
+    g_acc(3)
     g_sum(1)
     compute_h(2)
-    g_acc(3)
     rs_sum(0)
     rs_sum(1)
+    g_sum(2)
     g_acc(4)
-    g_sum(2)
     compute_h(3)
     ag_x()
+    ag_z()
     g_sum(3)
     g_sum(4)
-    ag_z()
     compute_h(4)
     grads_out(1)
     grads_out(0)
@@ -679,6 +676,15 @@
     gone(gpr, xss)
     gone(rss.at[pl.ds(0, 7)], rss_s)
     gone(agg.at[pl.ds(0, 7)], ags_s)
+
+
+def store(*refs):
+    sems = refs[8]
+    copies = [pltpu.make_async_copy(refs[i], refs[4 + i], sems.at[i]) for i in range(4)]
+    for d in copies:
+        d.start()
+    for d in copies:
+        d.wait()
 
 
 def shards(tokens, bti, ranks, w, down, up, cot):
@@ -723,10 +729,10 @@
             vm((ROUNDS, 2, rows, 256), BF),
             vm((ROUNDS, rows, 128), BF),
             vm((ROUNDS, rows, 128), BF),
-            vm((rows, 64), F32),
-            vm((2, half, 128), F32),
-            vm((8, 2, 24, 128), F32),
-            vm((8, 2, 24, 128), F32),
+            vm((rows, 128), F32),
+            vm((rows, 128), F32),
+            vm((8, 48, 128), F32),
+            vm((8, 48, 128), BF),
             vm((rows, 64), BF),
             vm((rows, 512), BF),
             vm((rows, 512), BF),
@@ -766,6 +772,15 @@
             collective_id=0, has_side_effects=True, vmem_limit_bytes=58 << 20
         ),
     )(bti, ranks, tokens, w, down, up, cot)
+    kept = [pltpu.with_memory_space_constraint(r, pltpu.VMEM) for r in (hid, gt, gd, gu)]
+    hid, gt, gd, gu = pl.pallas_call(
+        store,
+        out_shape=tuple(jax.ShapeDtypeStruct(r.shape, r.dtype) for r in kept),
+        in_specs=[out] * 4,
+        out_specs=[hbm] * 4,
+        scratch_shapes=[dma((4,))],
+        compiler_params=pltpu.CompilerParams(vmem_limit_bytes=1 << 20),
+    )(*kept)
     return hid, gt, gd.reshape(4, 64, ld), gu.reshape(4, 64, lf)
 
 

time: 110 us -> 105 us (0.955); the launches traced: 110 us -> 103 us
  local copies, waits for them, and re-layouts: 3.92 us -> 0 us
  Pallas kernels: 105 us -> 103 us
    pallas_call x1, Pallas kernels: 105 us -> 101 us  [shards(): pl.pallas_call(kernel, out_shape=(pltpu.VMEM((rows, lf), BF), pltpu.VMEM(...]
    unnamed x4 -> x0, local copies, waits for them, and re-layouts: 3.92 us -> none
    pallas_call x0 -> x1, Pallas kernels: none -> 2.1 us  [shards(): pl.pallas_call(store, out_shape=tuple((jax.ShapeDtypeStruct(r.shape, r.dt...]
where the time goes in v5:
time: 105 us; the launch traced here: 103 us
  Pallas kernels  103 us (98%)
    pallas_call x1, Pallas kernels, shards(): pl.pallas_call(kernel, out_shape=(pltpu.VMEM((rows, lf), BF), pltpu.VMEM(...  101 us

profile of v5, /device:TPU:1, one launch (start us, length us, event | category | flops | bytes accessed | tf_op | source)
XLA Modules:
  0.0 103.3 jit_solution(3249064007958445966)
XLA Ops:
  0.6 100.6 %shard_map.102 = (bf16[384,1792]{1,0:T(8,128)(2,1)S(1)}, bf16[384,640]{1,0:T(8,128)(2,1)S(1)}, f32[256,640]{1,0:T(8,128)S(1)}, f32[256,1792]{1,0:T(8,128)S(1)}) custom-call(s32[6]{0:T(128)} %bti.1, s32[8]{0:T(128)} %ranks.1, bf16[384,640]{1,0:T(8,128)(2,1)} %tok_h.1, bf16[5,64,1792]{2,1,0:T(8,128)(2,1)} %bitcast.6, bf16[64,5120]{1,0:T(8,128)(2,1)} %bitcast.7, ...), custom_call_target="tpu_custom_call" | custom-call | tf_op jit(solution)/shard_map/pallas_call | solution.py:702
  101.2 2.1 %shard_map.103 = (bf16[384,1792]{1,0:T(8,128)(2,1)}, bf16[384,640]{1,0:T(8,128)(2,1)}, f32[256,640]{1,0:T(8,128)}, f32[256,1792]{1,0:T(8,128)}) custom-call(bf16[384,1792]{1,0:T(8,128)(2,1)S(1)} %get-tuple-element.12.refs_0_, bf16[384,640]{1,0:T(8,128)(2,1)S(1)} %get-tuple-element.13.refs_1_, f32[256,640]{1,0:T(8,128)S(1)} %get-tuple-element.14.refs_2_, ...), custom_call_target="tpu_custom_call" | custom-call | tf_op jit(solution)/shard_map/pallas_call | solution.py:776

commit v6 on v5

--- a/solution.py
+++ b/solution.py
@@ -409,7 +409,7 @@
         each(lo, hi, body)
 
     fx, fz = f // 2, lax.rem(f, 2)
-    cols = (pl.ds(0, 896), pl.ds(896, 1536))
+    cols = (pl.ds(0, 1152), pl.ds(1152, 1280))
 
     def gx(p):
         go(gpart.at[1 - c, :, cols[p]], gpr.at[:, cols[p]], xss, xrs.at[p], partner)
@@ -455,31 +455,22 @@
         go(ref, ref, ags_s, ags_r.at[p, 1], fs("Z"))
         to_x(ref, ags_r.at[p, 0])
 
-    def ag_z():
-        got(agg.at[pl.ds(0, 3), :, cols[0]], ags_r.at[0, 0])
-        for r in range(1, 4):
-            ref = agg.at[lax.rem(f + 8 - 2 * r, 8), :, cols[0]]
-            go(ref, ref, ags_s, ags_r.at[0, 1], fs("Z"))
-
-    def ag_x():
-        ref = agg.at[fn["Z"], :, cols[1]]
-        got(ref, ags_r.at[1, 1])
-        to_x(ref, ags_r.at[1, 0])
+    def ag_x(p):
+        ref = agg.at[fn["Z"], :, cols[p]]
+        got(ref, ags_r.at[p, 1])
+        to_x(ref, ags_r.at[p, 0])
 
     def grads_out(p):
-        if p == 0:
-            got(agg.at[pl.ds(0, 4), :, cols[p]], ags_r.at[p, 1])
-        else:
-            got(agg.at[pl.ds(0, 6), :, cols[p]], ags_r.at[p, 0])
+        got(agg.at[pl.ds(0, 6), :, cols[p]], ags_r.at[p, 0])
 
         def body(k):
             at = pl.ds(pl.multiple_of(k * 32, 32), 32)
             v = agg[k, :, cols[p]].astype(F32)
             if p == 0:
                 gd_out[at, :] = v[:, :ld]
-                gu_out[at, 0:256] = v[:, ld:]
+                gu_out[at, 0:512] = v[:, ld:]
             else:
-                gu_out[at, 256:] = v
+                gu_out[at, 512:] = v
 
         each(0, 8, body)
 
@@ -597,11 +588,11 @@
     compact(1, tok, dall)
     each(1, 8, lambda k: b_desc(k).start())
     t_C(1)
+    t_B(1)
     w_E(0)
     b_sum()
     each(1, 8, lambda k: ag_desc(k).start())
     t_B(0)
-    t_B(1)
     w_A(4)
     w_D(1)
     x_C(2)
@@ -611,16 +602,16 @@
     w_B(3)
     w_C(3)
     grad_down_part()
-    grad_up_part(0, 1)
+    grad_up_part(0, 2)
     gx(0)
-    grad_up_part(1, 7)
+    grad_up_part(2, 7)
     gx(1)
     w_E(1)
-    t_D(0)
+    t_D(1)
     w_B(4)
     x_O(2)
     rs_z(0)
-    t_D(1)
+    t_D(0)
     w_P(1)
     compute_g(1)
     g_acc(0)
@@ -644,23 +635,23 @@
     g_sum(0)
     w_E(4)
     compute_h(1)
+    rs_sum(0)
     w_P(4)
     compute_g(4)
     g_acc(3)
+    rs_sum(1)
     g_sum(1)
     compute_h(2)
-    rs_sum(0)
-    rs_sum(1)
     g_sum(2)
+    ag_x(0)
     g_acc(4)
+    ag_x(1)
     compute_h(3)
-    ag_x()
-    ag_z()
     g_sum(3)
     g_sum(4)
     compute_h(4)
+    grads_out(0)
     grads_out(1)
-    grads_out(0)
     gt_final()
 
     gone(wall.at[:, pl.ds(0, 15 * SUB)], wss)

time: 105 us -> 102 us (0.971); the launches traced: 103 us -> 102 us
    pallas_call x1, Pallas kernels: 101 us -> 99.4 us  [shards(): pl.pallas_call(kernel, out_shape=(pltpu.VMEM((rows, lf), BF), pltpu.VMEM(...]
where the time goes in v6:
time: 102 us
  Pallas kernels  102 us (100%)
    pallas_call x1, Pallas kernels, shards(): pl.pallas_call(kernel, out_shape=(pltpu.VMEM((rows, lf), BF), pltpu.VMEM(...  99.4 us
    pallas_call x1, Pallas kernels, shards(): pl.pallas_call(store, out_shape=tuple((jax.ShapeDtypeStruct(r.shape, r.dt...  2.1 us

profile of v6, /device:TPU:1, one launch (start us, length us, event | category | flops | bytes accessed | tf_op | source)
XLA Modules:
  0.0 102.2 jit_solution(13355853901962674789)
XLA Ops:
  0.6 99.4 %shard_map.102 = (bf16[384,1792]{1,0:T(8,128)(2,1)S(1)}, bf16[384,640]{1,0:T(8,128)(2,1)S(1)}, f32[256,640]{1,0:T(8,128)S(1)}, f32[256,1792]{1,0:T(8,128)S(1)}) custom-call(s32[6]{0:T(128)} %bti.1, s32[8]{0:T(128)} %ranks.1, bf16[384,640]{1,0:T(8,128)(2,1)} %tok_h.1, bf16[5,64,1792]{2,1,0:T(8,128)(2,1)} %bitcast.6, bf16[64,5120]{1,0:T(8,128)(2,1)} %bitcast.7, ...), custom_call_target="tpu_custom_call" | custom-call | tf_op jit(solution)/shard_map/pallas_call | solution.py:693
  100.1 2.1 %shard_map.103 = (bf16[384,1792]{1,0:T(8,128)(2,1)}, bf16[384,640]{1,0:T(8,128)(2,1)}, f32[256,640]{1,0:T(8,128)}, f32[256,1792]{1,0:T(8,128)}) custom-call(bf16[384,1792]{1,0:T(8,128)(2,1)S(1)} %get-tuple-element.12.refs_0_, bf16[384,640]{1,0:T(8,128)(2,1)S(1)} %get-tuple-element.13.refs_1_, f32[256,640]{1,0:T(8,128)S(1)} %get-tuple-element.14.refs_2_, ...), custom_call_target="tpu_custom_call" | custom-call | tf_op jit(solution)/shard_map/pallas_call | solution.py:767

commit v7 on v6

--- a/solution.py
+++ b/solution.py
@@ -280,9 +280,8 @@
     def t_D(p):
         t_CD(p, "LZ", "RZ", 3, 4)
 
-    def t_E():
-        for p in range(2):
-            got(tokq.at[pl.ds(0, 2), tq[p]], trs.at[p, 5])
+    def t_E(p):
+        got(tokq.at[pl.ds(0, 2), tq[p]], trs.at[p, 5])
 
     def adapter(src, width, all_, relay, s):
         def own(ji, ci):
@@ -441,9 +440,15 @@
             at = (3 + r, slice(None), cols[p])
             go(rss.at[at], rsr.at[at], rss_s, rss_r.at[p, 1], fx_to(r))
 
-    def to_x(ref, sem):
-        for r in range(1, 4):
-            go(ref, ref, ags_s, sem, fx_to(r))
+    def to_x(ref, p, k):
+        go(ref, ref, ags_s, ags_r.at[p, k], fs("R"))
+        go(ref, ref, ags_s, ags_r.at[p, k + 1], fs("L"))
+
+    def on_x(p, left, right, k):
+        for name, e, to in ((left, 0, "R"), (right, 1, "L")):
+            got(agg.at[fn[name], :, cols[p]], ags_r.at[p, k + e])
+            ref = agg.at[fn[name], pl.ds(16 * e, 16), cols[p]]
+            go(ref, ref, ags_s, ags_r.at[p, 5], fs(to))
 
     def rs_sum(p):
         s = chunk(f, p) + rsr[fx, :, cols[p]].astype(F32)
@@ -452,16 +457,22 @@
             s = s + rsr[3 + r, :, cols[p]].astype(F32)
         agg[f, :, cols[p]] = s.astype(BF)
         ref = agg.at[f, :, cols[p]]
-        go(ref, ref, ags_s, ags_r.at[p, 1], fs("Z"))
-        to_x(ref, ags_r.at[p, 0])
+        go(ref, ref, ags_s, ags_r.at[p, 2], fs("Z"))
+        to_x(ref, p, 0)
 
     def ag_x(p):
         ref = agg.at[fn["Z"], :, cols[p]]
-        got(ref, ags_r.at[p, 1])
-        to_x(ref, ags_r.at[p, 0])
+        got(ref, ags_r.at[p, 2])
+        to_x(ref, p, 3)
+
+    def ag_o(p):
+        on_x(p, "L", "R", 0)
+
+    def ag_oz(p):
+        on_x(p, "LZ", "RZ", 3)
 
     def grads_out(p):
-        got(agg.at[pl.ds(0, 6), :, cols[p]], ags_r.at[p, 0])
+        got(agg.at[pl.ds(0, 2), :, cols[p]], ags_r.at[p, 5])
 
         def body(k):
             at = pl.ds(pl.multiple_of(k * 32, 32), 32)
@@ -556,16 +567,16 @@
 
         each(0, 6, body)
 
+    pl.semaphore_wait(barrier, 16)
+    u_cross()
+    u_own()
+    wloc.wait()
+    w_A(0)
+    w_A(1)
     t_make()
+    t_A(0)
     dq_make()
     make_gain()
-    wloc.wait()
-    pl.semaphore_wait(barrier, 16)
-    w_A(0)
-    u_cross()
-    u_own()
-    w_A(1)
-    t_A(0)
     w_B(0)
     w_C(0)
     w_A(2)
@@ -607,11 +618,11 @@
     grad_up_part(2, 7)
     gx(1)
     w_E(1)
-    t_D(1)
     w_B(4)
     x_O(2)
     rs_z(0)
     t_D(0)
+    t_D(1)
     w_P(1)
     compute_g(1)
     g_acc(0)
@@ -624,7 +635,8 @@
     compute_g(2)
     g_acc(1)
     w_D(4)
-    t_E()
+    t_E(0)
+    t_E(1)
     compute_h(0)
     w_E(3)
     rs_x(0)
@@ -642,13 +654,17 @@
     rs_sum(1)
     g_sum(1)
     compute_h(2)
+    ag_o(0)
     g_sum(2)
     ag_x(0)
     g_acc(4)
     ag_x(1)
     compute_h(3)
+    ag_o(1)
     g_sum(3)
     g_sum(4)
+    ag_oz(0)
+    ag_oz(1)
     compute_h(4)
     grads_out(0)
     grads_out(1)
@@ -757,7 +773,7 @@
             dma,
             dma((2, 2)),
             dma,
-            dma((2, 2)),
+            dma((2, 6)),
         ],
         compiler_params=pltpu.CompilerParams(
             collective_id=0, has_side_effects=True, vmem_limit_bytes=58 << 20

time: 102 us -> 101 us (level)
  no operation moved by 1% of the time
where the time goes in v7:
time: 101 us
  Pallas kernels  101 us (100%)
    pallas_call x1, Pallas kernels, shards(): pl.pallas_call(kernel, out_shape=(pltpu.VMEM((rows, lf), BF), pltpu.VMEM(...  98.6 us
    pallas_call x1, Pallas kernels, shards(): pl.pallas_call(store, out_shape=tuple((jax.ShapeDtypeStruct(r.shape, r.dt...  2.1 us

profile of v7, /device:TPU:1, one launch (start us, length us, event | category | flops | bytes accessed | tf_op | source)
XLA Modules:
  0.0 101.3 jit_solution(4673206760706441525)
XLA Ops:
  0.6 98.6 %shard_map.102 = (bf16[384,1792]{1,0:T(8,128)(2,1)S(1)}, bf16[384,640]{1,0:T(8,128)(2,1)S(1)}, f32[256,640]{1,0:T(8,128)S(1)}, f32[256,1792]{1,0:T(8,128)S(1)}) custom-call(s32[6]{0:T(128)} %bti.1, s32[8]{0:T(128)} %ranks.1, bf16[384,640]{1,0:T(8,128)(2,1)} %tok_h.1, bf16[5,64,1792]{2,1,0:T(8,128)(2,1)} %bitcast.6, bf16[64,5120]{1,0:T(8,128)(2,1)} %bitcast.7, ...), custom_call_target="tpu_custom_call" | custom-call | tf_op jit(solution)/shard_map/pallas_call | solution.py:709
  99.2 2.1 %shard_map.103 = (bf16[384,1792]{1,0:T(8,128)(2,1)}, bf16[384,640]{1,0:T(8,128)(2,1)}, f32[256,640]{1,0:T(8,128)}, f32[256,1792]{1,0:T(8,128)}) custom-call(bf16[384,1792]{1,0:T(8,128)(2,1)S(1)} %get-tuple-element.12.refs_0_, bf16[384,640]{1,0:T(8,128)(2,1)S(1)} %get-tuple-element.13.refs_1_, f32[256,640]{1,0:T(8,128)S(1)} %get-tuple-element.14.refs_2_, ...), custom_call_target="tpu_custom_call" | custom-call | tf_op jit(solution)/shard_map/pallas_call | solution.py:783

commit v8 on v7

--- a/solution.py
+++ b/solution.py
@@ -408,7 +408,7 @@
         each(lo, hi, body)
 
     fx, fz = f // 2, lax.rem(f, 2)
-    cols = (pl.ds(0, 1152), pl.ds(1152, 1280))
+    cols = (pl.ds(0, 1408), pl.ds(1408, 1024))
 
     def gx(p):
         go(gpart.at[1 - c, :, cols[p]], gpr.at[:, cols[p]], xss, xrs.at[p], partner)
@@ -479,9 +479,9 @@
             v = agg[k, :, cols[p]].astype(F32)
             if p == 0:
                 gd_out[at, :] = v[:, :ld]
-                gu_out[at, 0:512] = v[:, ld:]
+                gu_out[at, 0:768] = v[:, ld:]
             else:
-                gu_out[at, 512:] = v
+                gu_out[at, 768:] = v
 
         each(0, 8, body)
 
@@ -613,9 +613,9 @@
     w_B(3)
     w_C(3)
     grad_down_part()
-    grad_up_part(0, 2)
+    grad_up_part(0, 3)
     gx(0)
-    grad_up_part(2, 7)
+    grad_up_part(3, 7)
     gx(1)
     w_E(1)
     w_B(4)

time: 101 us -> 101 us (level); the launches traced: 101 us -> 99.7 us
  Pallas kernels: 101 us -> 99 us
    pallas_call x1, Pallas kernels: 98.6 us -> 96.9 us  [shards(): pl.pallas_call(kernel, out_shape=(pltpu.VMEM((rows, lf), BF), pltpu.VMEM(...]
where the time goes in v8:
time: 101 us; the launch traced here: 99.7 us
  Pallas kernels  99 us (98%)
    pallas_call x1, Pallas kernels, shards(): pl.pallas_call(kernel, out_shape=(pltpu.VMEM((rows, lf), BF), pltpu.VMEM(...  96.9 us
    pallas_call x1, Pallas kernels, shards(): pl.pallas_call(store, out_shape=tuple((jax.ShapeDtypeStruct(r.shape, r.dt...  2.1 us

profile of v8, /device:TPU:1, one launch (start us, length us, event | category | flops | bytes accessed | tf_op | source)
XLA Modules:
  0.0 99.7 jit_solution(5347994535085845630)
XLA Ops:
  0.6 96.9 %shard_map.102 = (bf16[384,1792]{1,0:T(8,128)(2,1)S(1)}, bf16[384,640]{1,0:T(8,128)(2,1)S(1)}, f32[256,640]{1,0:T(8,128)S(1)}, f32[256,1792]{1,0:T(8,128)S(1)}) custom-call(s32[6]{0:T(128)} %bti.1, s32[8]{0:T(128)} %ranks.1, bf16[384,640]{1,0:T(8,128)(2,1)} %tok_h.1, bf16[5,64,1792]{2,1,0:T(8,128)(2,1)} %bitcast.6, bf16[64,5120]{1,0:T(8,128)(2,1)} %bitcast.7, ...), custom_call_target="tpu_custom_call" | custom-call | tf_op jit(solution)/shard_map/pallas_call | solution.py:709
  97.6 2.1 %shard_map.103 = (bf16[384,1792]{1,0:T(8,128)(2,1)}, bf16[384,640]{1,0:T(8,128)(2,1)}, f32[256,640]{1,0:T(8,128)}, f32[256,1792]{1,0:T(8,128)}) custom-call(bf16[384,1792]{1,0:T(8,128)(2,1)S(1)} %get-tuple-element.12.refs_0_, bf16[384,640]{1,0:T(8,128)(2,1)S(1)} %get-tuple-element.13.refs_1_, f32[256,640]{1,0:T(8,128)S(1)} %get-tuple-element.14.refs_2_, ...), custom_call_target="tpu_custom_call" | custom-call | tf_op jit(solution)/shard_map/pallas_call | solution.py:783

commit v9 on v8

--- a/solution.py
+++ b/solution.py
@@ -643,9 +643,9 @@
     w_P(3)
     compute_g(3)
     g_acc(2)
-    rs_x(1)
     g_sum(0)
     w_E(4)
+    rs_x(1)
     compute_h(1)
     rs_sum(0)
     w_P(4)

time: 101 us -> 101 us (level)
  no operation moved by 1% of the time
where the time goes in v9:
time: 101 us; the launch traced here: 99.6 us
  Pallas kernels  99 us (98%)
    pallas_call x1, Pallas kernels, shards(): pl.pallas_call(kernel, out_shape=(pltpu.VMEM((rows, lf), BF), pltpu.VMEM(...  96.9 us
    pallas_call x1, Pallas kernels, shards(): pl.pallas_call(store, out_shape=tuple((jax.ShapeDtypeStruct(r.shape, r.dt...  2.1 us

profile of v9, /device:TPU:1, one launch (start us, length us, event | category | flops | bytes accessed | tf_op | source)
XLA Modules:
  0.0 99.6 jit_solution(7274371396737885731)
XLA Ops:
  0.6 96.9 %shard_map.102 = (bf16[384,1792]{1,0:T(8,128)(2,1)S(1)}, bf16[384,640]{1,0:T(8,128)(2,1)S(1)}, f32[256,640]{1,0:T(8,128)S(1)}, f32[256,1792]{1,0:T(8,128)S(1)}) custom-call(s32[6]{0:T(128)} %bti.1, s32[8]{0:T(128)} %ranks.1, bf16[384,640]{1,0:T(8,128)(2,1)} %tok_h.1, bf16[5,64,1792]{2,1,0:T(8,128)(2,1)} %bitcast.6, bf16[64,5120]{1,0:T(8,128)(2,1)} %bitcast.7, ...), custom_call_target="tpu_custom_call" | custom-call | tf_op jit(solution)/shard_map/pallas_call | solution.py:709
  97.5 2.1 %shard_map.103 = (bf16[384,1792]{1,0:T(8,128)(2,1)}, bf16[384,640]{1,0:T(8,128)(2,1)}, f32[256,640]{1,0:T(8,128)}, f32[256,1792]{1,0:T(8,128)}) custom-call(bf16[384,1792]{1,0:T(8,128)(2,1)S(1)} %get-tuple-element.12.refs_0_, bf16[384,640]{1,0:T(8,128)(2,1)S(1)} %get-tuple-element.13.refs_1_, f32[256,640]{1,0:T(8,128)S(1)} %get-tuple-element.14.refs_2_, ...), custom_call_target="tpu_custom_call" | custom-call | tf_op jit(solution)/shard_map/pallas_call | solution.py:783
